TPU v7x, 32 devices: a whole 2x2x4 slice. The times are simulated.
32 devices in a mesh: dp: 2 (over x), tp: 4 (over z), dm: 4 (over y, core).
Axes of the slice: x: 2, y: 2, z: 4, core: 2. Of those that a mesh axis runs over, the one named last changes fastest.
Arguments:
- tokens: bfloat16 [8192, 3584], P('dp', 'dm'), parts along dimension 0
- positions: int32 [8, 1024], P('dp'), parts along dimension 0
- norm_pre_attn: bfloat16 [3584], P('dm')
- w_query: bfloat16 [3584, 16, 256], P('dm', 'tp')
- w_key: bfloat16 [3584, 8, 256], P('dm', 'tp')
- w_value: bfloat16 [3584, 8, 256], P('dm', 'tp')
- w_out: bfloat16 [16, 256, 3584], P('tp', None, 'dm')
- norm_post_attn: bfloat16 [3584], P('dm')
- norm_pre_ffw: bfloat16 [3584], P('dm')
- w_gate: bfloat16 [3584, 14336], P('dm', 'tp')
- w_up: bfloat16 [3584, 14336], P('dm', 'tp')
- w_down: bfloat16 [14336, 3584], P('tp', 'dm')
- norm_post_ffw: bfloat16 [3584], P('dm')
Outputs:
- output 1: bfloat16 [8192, 3584], P('dp', 'dm'), parts along dimension 0
- output 2: bfloat16 [8192, 8, 256], P('dp', 'tp'), parts along dimension 0
- output 3: bfloat16 [8192, 8, 256], P('dp', 'tp'), parts along dimension 0
There are 2 independent parts. A program takes and returns all parts, laid end to end along the dimension named above; an argument that names none is the same for every part.
All inputs are finite; a program needn't handle non-finite values.
Results may differ from a plain program's by a relative error of at most 0.02.
Values are sent between devices in bfloat16 or wider.
A program may use at most 1 GiB of HBM per device.

v0:
```python
import jax
import jax.numpy as jnp
from jax import lax
from jax.sharding import PartitionSpec as P

NORM_EPS = 1e-6
SOFT_CAP = 50.0
ROPE_BASE = 10000.0
WINDOW_LEN = 4096


def norm_group(values, gain_vec, model_dim):
    vals32 = values.astype(jnp.float32)
    sq_sum = lax.psum(jnp.sum(vals32 * vals32, axis=-1, keepdims=True), 'dm')
    return vals32 * lax.rsqrt(sq_sum / model_dim + NORM_EPS) * (1.0 + gain_vec.astype(jnp.float32))


def rotary_tables(positions, head_dim):
    half_dim = head_dim // 2
    inv_freq = ROPE_BASE ** (-2.0 * jnp.arange(half_dim, dtype=jnp.float32) / head_dim)
    angles = positions.reshape(-1).astype(jnp.float32)[:, None] * inv_freq[None, :]
    return jnp.cos(angles)[:, None, :], jnp.sin(angles)[:, None, :]


def apply_rotary(head_vals, cos_tab, sin_tab):
    half_dim = head_vals.shape[-1] // 2
    lower_half = head_vals[..., :half_dim].astype(jnp.float32)
    upper_half = head_vals[..., half_dim:].astype(jnp.float32)
    rotated = jnp.concatenate([lower_half * cos_tab - upper_half * sin_tab, upper_half * cos_tab + lower_half * sin_tab], axis=-1)
    return rotated.astype(jnp.bfloat16)


def attend(query_rows, key_rows, value_rows, positions, score_scale):
    num_seqs, seq_len, kv_heads, group_size, head_dim = query_rows.shape
    query_block = min(seq_len, 256)
    key_index = jnp.arange(seq_len)

    def one_block(block_index):
        row_start = block_index * query_block
        q_blk = lax.dynamic_slice_in_dim(query_rows, row_start, query_block, axis=1)
        q_pos = lax.dynamic_slice_in_dim(positions, row_start, query_block, axis=1)
        scores = jnp.einsum('bqkgd,bskd->bkgqs', q_blk, key_rows, preferred_element_type=jnp.float32) * score_scale
        scores = SOFT_CAP * jnp.tanh(scores / SOFT_CAP)
        q_index = row_start + jnp.arange(query_block)
        allowed = (key_index[None, :] <= q_index[:, None])[None] & (q_pos[:, :, None] - positions[:, None, :] < WINDOW_LEN)
        scores = jnp.where(allowed[:, None, None], scores, -1e30)
        attn_probs = jax.nn.softmax(scores, axis=-1).astype(jnp.bfloat16)
        return jnp.einsum('bkgqs,bskd->bqkgd', attn_probs, value_rows, preferred_element_type=jnp.float32).astype(jnp.bfloat16)

    blocks = lax.map(one_block, jnp.arange(seq_len // query_block))
    return jnp.moveaxis(blocks, 0, 1).reshape(num_seqs * seq_len, kv_heads * group_size, head_dim)


def solution(mesh):
    dm_size = mesh.shape['dm']
    tp_size = mesh.shape['tp']

    def layer(tokens, positions, norm_pre_attn, w_query, w_key, w_value, w_out, norm_post_attn, norm_pre_ffw, w_gate, w_up, w_down, norm_post_ffw):
        model_dim = tokens.shape[1] * dm_size
        heads_local, head_dim = w_query.shape[1], w_query.shape[2]
        kv_local = w_key.shape[1]
        num_seqs, seq_len = positions.shape
        score_scale = (model_dim / (heads_local * tp_size)) ** -0.5
        normed = norm_group(tokens, norm_pre_attn, model_dim).astype(jnp.bfloat16)
        query_part = jnp.einsum('nd,dhk->nhk', normed, w_query, preferred_element_type=jnp.float32).astype(jnp.bfloat16)
        key_part = jnp.einsum('nd,dhk->nhk', normed, w_key, preferred_element_type=jnp.float32).astype(jnp.bfloat16)
        value_part = jnp.einsum('nd,dhk->nhk', normed, w_value, preferred_element_type=jnp.float32).astype(jnp.bfloat16)
        query_rows, key_rows, value_rows = lax.psum((query_part, key_part, value_part), 'dm')
        cos_tab, sin_tab = rotary_tables(positions, head_dim)
        query_rows = apply_rotary(query_rows, cos_tab, sin_tab)
        key_rows = apply_rotary(key_rows, cos_tab, sin_tab)
        group_size = heads_local // kv_local
        attn_rows = attend(query_rows.reshape(num_seqs, seq_len, kv_local, group_size, head_dim), key_rows.reshape(num_seqs, seq_len, kv_local, head_dim), value_rows.reshape(num_seqs, seq_len, kv_local, head_dim), positions, score_scale)
        out_part = jnp.einsum('nhk,hkd->nd', attn_rows, w_out, preferred_element_type=jnp.float32).astype(jnp.bfloat16)
        attn_out = lax.psum(out_part, 'tp')
        hidden = (tokens.astype(jnp.float32) + norm_group(attn_out, norm_post_attn, model_dim)).astype(jnp.bfloat16)
        ffw_in = norm_group(hidden, norm_pre_ffw, model_dim).astype(jnp.bfloat16)
        gate_part = jnp.dot(ffw_in, w_gate, preferred_element_type=jnp.float32).astype(jnp.bfloat16)
        up_part = jnp.dot(ffw_in, w_up, preferred_element_type=jnp.float32).astype(jnp.bfloat16)
        gate_proj, up_proj = lax.psum((gate_part, up_part), 'dm')
        gated_act = (jax.nn.gelu(gate_proj.astype(jnp.float32), approximate=True) * up_proj.astype(jnp.float32)).astype(jnp.bfloat16)
        down_part = jnp.dot(gated_act, w_down, preferred_element_type=jnp.float32).astype(jnp.bfloat16)
        down_proj = lax.psum(down_part, 'tp')
        tokens_out = (hidden.astype(jnp.float32) + norm_group(down_proj, norm_post_ffw, model_dim)).astype(jnp.bfloat16)
        return tokens_out, key_rows, value_rows

    width_spec = P('dm')
    in_specs = (P('dp', 'dm'), P('dp', None), width_spec, P('dm', 'tp', None), P('dm', 'tp', None), P('dm', 'tp', None), P('tp', None, 'dm'), width_spec, width_spec, P('dm', 'tp'), P('dm', 'tp'), P('tp', 'dm'), width_spec)
    out_specs = (P('dp', 'dm'), P('dp', 'tp', None), P('dp', 'tp', None))
    return jax.shard_map(layer, mesh=mesh, in_specs=in_specs, out_specs=out_specs, check_vma=False)
```

profile of v0, /device:TPU:0, one launch (start us, length us, event | category | flops | bytes accessed | tf_op | source)
XLA Modules:
  0.0 2242.9 jit_solution(18298216082363692623)
XLA Ops:
  7.2 4.7 fusion.35
  11.9 12.7 psum.77
  25.4 14.6 convolution_convert_fusion.2
  40.0 6.5 convolution_convert_fusion.3
  46.5 6.4 convolution_convert_fusion.4
  52.9 11.8 all-reduce.7.cloned.1.call-start
  64.8 9.3 multiply_cosine_fusion
  74.2 267.4 %all-reduce.13.cloned.1.call-done = (bf16[4096,4,256]{2,0,1:T(8,128)(2,1)}, bf16[4096,2,256]{2,0,1:T(8,128)(2,1)}, bf16[4096,2,256]{2,0,1:T(8,128)(2,1)}) async-done(((bf16[4096,4,256]{2,0,1:T(8,128)(2,1)}, bf16[4096,2,256]{2,0,1:T(8,128)(2,1)}, bf16[4096,2,256]{2,0,1:T(8,128)(2,1)}), (bf16[4096,4,256]{2,0,1:T(8,128)(2,1)}, bf16[4096,2,256]{2,0,1:T(8,128)(2,1)}, ...) | async-done | bytes 16777232 | tf_op jit(solution)/shard_map/psum | solution.py:68
  341.5 4.3 fusion.52
  346.3 2.3 copy.40
  351.0 1.2 slice-done.1
  352.2 4.0 fusion.44
  356.2 2.3 copy.33
  358.5 6.5 pad_maximum_fusion
  365.1 200.1 %while.13 = (s32[]{:T(128)}, bf16[4,4,256,2,2,256]{5,2,0,1,4,3:T(8,128)(2,1)}, s32[4]{0:T(128)S(1)}, s32[4,1024]{1,0:T(4,128)S(1)}, bf16[4,1024,2,2,256]{4,1,0,3...) while((s32[]{:T(128)}, ...), condition=%wide.region_8.9_spmd.clone, body=%wide.region_5.8_spmd.clone.sunk | while | flops 4341367808 | bytes 86571696 | solution.py:50
  367.5 10.9 fusion.83
  378.4 22.9 %fusion.85 = (f32[4,2,2,256]{3,2,1,0:T(2,128)S(1)}, f32[4,2,2,256,1024]{4,3,2,1,0:T(8,128)}) fusion(f32[4,2,256,2,1024]{4,2,3,1,0:T(8,128)} %fusion.83, pred[4,256,1024]{2,1,0:T(8,128)(4,1)S(1)} %fusion.84), kind=kOutput, calls=%fused_computation.109.clone.1 | output fusion | flops 33555456 | bytes 34619392 | tf_op jit(solution)/shard_map/while/body/eval_jaxpr/sub | solution.py:47
  401.4 10.7 convert_bitcast_fusion.3
  412.0 3.0 copy_dynamic-update-slice_fusion.2
  417.5 10.9 fusion.83
  428.5 22.9 %fusion.85 = (f32[4,2,2,256]{3,2,1,0:T(2,128)S(1)}, f32[4,2,2,256,1024]{4,3,2,1,0:T(8,128)}) fusion(f32[4,2,256,2,1024]{4,2,3,1,0:T(8,128)} %fusion.83, pred[4,256,1024]{2,1,0:T(8,128)(4,1)S(1)} %fusion.84), kind=kOutput, calls=%fused_computation.109.clone.1 | output fusion | flops 33555456 | bytes 34619392 | tf_op jit(solution)/shard_map/while/body/eval_jaxpr/sub | solution.py:47
  451.4 10.7 convert_bitcast_fusion.3
  462.1 3.1 copy_dynamic-update-slice_fusion.2
  467.6 10.9 fusion.83
  478.5 22.9 %fusion.85 = (f32[4,2,2,256]{3,2,1,0:T(2,128)S(1)}, f32[4,2,2,256,1024]{4,3,2,1,0:T(8,128)}) fusion(f32[4,2,256,2,1024]{4,2,3,1,0:T(8,128)} %fusion.83, pred[4,256,1024]{2,1,0:T(8,128)(4,1)S(1)} %fusion.84), kind=kOutput, calls=%fused_computation.109.clone.1 | output fusion | flops 33555456 | bytes 34619392 | tf_op jit(solution)/shard_map/while/body/eval_jaxpr/sub | solution.py:47
  501.4 10.7 convert_bitcast_fusion.3
  512.1 3.1 copy_dynamic-update-slice_fusion.2
  517.6 10.9 fusion.83
  528.5 22.9 %fusion.85 = (f32[4,2,2,256]{3,2,1,0:T(2,128)S(1)}, f32[4,2,2,256,1024]{4,3,2,1,0:T(8,128)}) fusion(f32[4,2,256,2,1024]{4,2,3,1,0:T(8,128)} %fusion.83, pred[4,256,1024]{2,1,0:T(8,128)(4,1)S(1)} %fusion.84), kind=kOutput, calls=%fused_computation.109.clone.1 | output fusion | flops 33555456 | bytes 34619392 | tf_op jit(solution)/shard_map/while/body/eval_jaxpr/sub | solution.py:47
  551.5 10.7 convert_bitcast_fusion.3
  562.1 3.1 copy_dynamic-update-slice_fusion.2
  565.2 13.9 bitcast_convert_fusion
  579.2 255.8 %all-reduce.7.cloned.1.call-done = bf16[4096,896]{1,0:T(8,128)(2,1)} async-done(((bf16[4096,896]{1,0:T(8,128)(2,1)}), bf16[4096,896]{1,0:T(8,128)(2,1)}) %all-reduce.7.cloned.1.call-update) | async-done | bytes 7340048 | tf_op jit(solution)/shard_map/psum | solution.py:75
  835.1 4.6 fusion.31
  839.7 10.5 psum.82
  850.2 10.0 fusion.39
  860.3 10.5 psum.83
  870.8 37.7 %convolution_convert_fusion = bf16[4096,3584]{1,0:T(8,128)(2,1)} fusion(bf16[896,3584]{1,0:T(8,128)(2,1)} %param.25, bf16[4096,896]{1,0:T(8,128)(2,1)} %get-tuple-element.161, f32[896]{0:T(1024)S(1)} %convert_add_fusion.4, f32[4096]{0:T(1024)S(1)} %bitcast.88), kind=kOutput, calls=%fused_computation.39 | convolution fusion | flops 26336034816 | bytes 43142656 | tf_op jit(solution)/shard_map/dot_general | solution.py:79
  908.5 37.6 %convolution_convert_fusion.1 = bf16[4096,3584]{1,0:T(8,128)(2,1)} fusion(bf16[896,3584]{1,0:T(8,128)(2,1)} %param.24, bf16[4096,896]{1,0:T(8,128)(2,1)S(1)} %copy-done.3, f32[896]{0:T(1024)S(1)} %convert_add_fusion.4, f32[4096]{0:T(1024)S(1)} %bitcast.89), kind=kOutput, calls=%fused_computation.40 | convolution fusion | flops 26336034816 | bytes 43142656 | tf_op jit(solution)/shard_map/dot_general | solution.py:78
  946.2 961.1 %all-reduce.11.cloned.1.call-done = (bf16[4096,3584]{1,0:T(8,128)(2,1)}, bf16[4096,3584]{1,0:T(8,128)(2,1)}) async-done(((bf16[4096,3584]{1,0:T(8,128)(2,1)}, bf16[4096,3584]{1,0:T(8,128)(2,1)}), (bf16[4096,3584]{1,0:T(8,128)(2,1)}, bf16[4096,3584]{1,0:T(8,128)(2,1)})) %all-reduce.11.cloned.1.call-update) | async-done | bytes 58720272 | tf_op jit(solution)/shard_map/psum | solution.py:80
  1907.4 48.0 %fusion.48 = bf16[4096,896]{1,0:T(8,128)(2,1)} fusion(bf16[3584,896]{1,0:T(8,128)(2,1)} %param.26, bf16[4096,3584]{1,0:T(8,128)(2,1)} %get-tuple-element.155, bf16[4096,3584]{1,0:T(8,128)(2,1)} %get-tuple-element.156), kind=kOutput, calls=%fused_computation.76 | convolution fusion | flops 26486505472 | bytes 72482816 | tf_op jit(solution)/shard_map/dot_general | solution.py:82
  1955.4 10.1 copy.36
  1965.5 2.7 pad_maximum_fusion.2
  1968.2 27.4 %copy.35 = bf16[4096,2,256]{2,1,0:T(2,128)(2,1)} copy(bf16[4096,2,256]{2,0,1:T(8,128)(2,1)S(1)} %pad_maximum_fusion.2) | data formatting | bytes 8388608
  1995.6 216.0 %all-reduce.9.cloned.1.call-done = bf16[4096,896]{1,0:T(8,128)(2,1)} async-done(((bf16[4096,896]{1,0:T(8,128)(2,1)}), bf16[4096,896]{1,0:T(8,128)(2,1)}) %all-reduce.9.cloned.1.call-update) | async-done | bytes 7340048 | tf_op jit(solution)/shard_map/psum | solution.py:83
  2211.6 4.6 fusion.33
  2216.2 10.5 psum.87
  2226.7 9.4 fusion.42
  (75 shorter events, 10.9 us)
Async XLA Ops:
  7.2 18.2 copy-start
  7.2 334.3 %all-reduce.13.cloned.1.call-start = ((), (), s32[]{:S(2)}) async-start(), calls=%async_computation.3 | async-start | bytes 33554432 | tf_op jit(solution)/shard_map/psum | solution.py:68
  25.4 14.6 copy-start.2
  25.4 14.6 copy-start.13
  40.0 6.5 copy-start.14
  52.9 11.9 copy-start.9
  52.9 782.1 %all-reduce.7.cloned.1.call-start = ((), (), s32[]{:S(2)}) async-start(), calls=%async_computation | async-start | bytes 14680064 | tf_op jit(solution)/shard_map/psum | solution.py:75
  341.5 8.4 slice-start
  345.8 3.1 copy-start.6
  345.8 4.1 copy-start.7
  345.8 4.1 copy-start.4
  345.8 5.2 copy-start.5
  345.8 6.4 slice-start.1
  352.2 4.0 copy-start.8
  565.2 14.0 copy-start.10
  565.2 14.0 copy-start.11
  579.1 1328.2 %all-reduce.11.cloned.1.call-start = ((), (), s32[]{:S(2)}) async-start(), calls=%async_computation.2 | async-start | bytes 117440512 | tf_op jit(solution)/shard_map/psum | solution.py:80
  870.8 37.7 %copy-start.3 = (bf16[4096,896]{1,0:T(8,128)(2,1)S(1)}, bf16[4096,896]{1,0:T(8,128)(2,1)}, u32[]{:S(2)}) copy-start(bf16[4096,896]{1,0:T(8,128)(2,1)} %get-tuple-element.161) | copy-start | bytes 22020100
  946.2 1265.4 %all-reduce.9.cloned.1.call-start = ((), (), s32[]{:S(2)}) async-start(), calls=%async_computation.1 | async-start | bytes 14680064 | tf_op jit(solution)/shard_map/psum | solution.py:83
  1907.4 48.0 %copy-start.12 = (bf16[896]{0:T(1024)(128)(2,1)S(1)}, bf16[896]{0:T(1024)(128)(2,1)}, u32[]{:S(2)}) copy-start(bf16[896]{0:T(1024)(128)(2,1)} %param.27) | copy-start | bytes 5380
  2226.7 9.4 copy-start.1
Sparse Core Ops, SparseCore 0:
  53.1 288.4 all-reduce.12
  579.3 255.7 all-reduce.6
  946.3 961.0 all-reduce.10
  1955.5 256.0 all-reduce.8
where the time goes:
time: 2250 us; the launch traced here: 2240 us
  waiting for transfers between devices  1700 us (76%)
  matrix products  251 us (11%)
  other arithmetic  158 us (7%)
  local copies, waits for them, and re-layouts  60.3 us (3%)
  blocking collectives  44.3 us (2%)
    psum x1, waiting for transfers between devices, layer(): gate_proj, up_proj = lax.psum((gate_part, up_part), 'dm')  961 us
    psum x1, waiting for transfers between devices, layer(): lax.psum((query_part, key_part, value_part), 'dm')  267 us
    psum x1, waiting for transfers between devices, layer(): attn_out = lax.psum(out_part, 'tp')  256 us
    psum x1, waiting for transfers between devices, layer(): down_proj = lax.psum(down_part, 'tp')  216 us
    sub x4, other arithmetic, one_block(): attn_probs = jax.nn.softmax(scores, axis=-1).astype(jnp.bfloat16)  91.8 us
    dot_general x1, matrix products, layer(): jnp.dot(gated_act, w_down, preferred_element_type=jnp.float32)  48 us
  transfers between devices with their start and end apart: 4, of which 4 were waited for; matrix products, arithmetic and copies ran while one was open for 2% of the time, Pallas kernels for 0%

commit v1 on v0

v1 whole, which is shorter than its diff:
```python
import functools

import jax
import jax.numpy as jnp
from jax import lax
from jax.experimental import pallas as pl
from jax.experimental.pallas import tpu as pltpu
from jax.sharding import PartitionSpec as P

NORM_EPS = 1e-6
SOFT_CAP = 50.0
ROPE_BASE = 10000.0
WINDOW_LEN = 4096
BF16 = jnp.bfloat16
F32 = jnp.float32

CHUNK = 32
LAG = 2
LINE = 4
VMEM_BYTES = 60 * 1024 * 1024

ANY = pl.BlockSpec(memory_space=pl.ANY)
VMEM = pl.BlockSpec(memory_space=pltpu.VMEM)
DMA = pltpu.SemaphoreType.DMA


def places():
    row = lax.axis_index('dp')
    line = lax.axis_index('tp')
    me = lax.axis_index('dm')
    side = lax.div(me, 2)
    core = me - 2 * side
    return row, line, me, 2 * side + 1 - core, 2 * (1 - side) + core, 2 * (1 - side) + 1 - core


def remote(src, dst, send_sem, recv_sem, device):
    return pltpu.make_async_remote_copy(src_ref=src, dst_ref=dst, send_sem=send_sem, recv_sem=recv_sem, device_id=device, device_id_type=pl.DeviceIdType.MESH)


def meet(peers):
    barrier = pltpu.get_barrier_semaphore()
    for peer in peers:
        pl.semaphore_signal(barrier, inc=1, device_id=peer, device_id_type=pl.DeviceIdType.MESH)
    pl.semaphore_wait(barrier, len(peers))


def line_peers(line):
    return [{'tp': lax.rem(line + 1, LINE)}, {'tp': lax.rem(line + LINE - 1, LINE)}]


class Shard:
    def __init__(self, src, dst, by_rows, pieces):
        self.src, self.dst, self.by_rows, self.pieces = src, dst, by_rows, pieces
        self.rows = src.shape[0]
        self.unit = self.rows // (2 * pieces)

    def own(self, half, piece):
        return self.src.at[pl.ds(pl.multiple_of((half * self.pieces + piece) * self.unit, self.unit), self.unit)]

    def at(self, shard, half, piece):
        start = (half * self.pieces + piece) * self.unit
        if self.by_rows:
            return self.dst.at[pl.ds(pl.multiple_of(shard * self.rows + start, self.unit), self.unit)]
        cols = self.src.shape[1]
        return self.dst.at[pl.ds(pl.multiple_of(start, self.unit), self.unit), pl.ds(pl.multiple_of(shard * cols, cols), cols)]

    def whole(self, shard):
        if self.by_rows:
            return self.dst.at[pl.ds(pl.multiple_of(shard * self.rows, self.rows), self.rows)]
        cols = self.src.shape[1]
        return self.dst.at[:, pl.ds(pl.multiple_of(shard * cols, cols), cols)]


class WeightGather:
    def __init__(self, shards, own_send, own_recv, send, recv):
        self.shards, self.own_send, self.own_recv, self.send, self.recv = shards, own_send, own_recv, send, recv
        self.row, _, self.me, self.mate, self.across, self.cross = places()
        self.units = [(w, p) for w in range(len(shards)) for p in range(shards[w].pieces)]

    def copy(self, k, hop):
        w, p = self.units[k]
        shard = self.shards[w]
        mine, other = self.row, 1 - self.row
        if hop == 0:
            src, dst, device = shard.own(mine, p), shard.at(self.me, mine, p), {'dm': self.across}
        elif hop == 1:
            src = dst = shard.at(self.across, mine, p)
            device = {'dp': other}
        elif hop == 2:
            src = dst = shard.at(self.across, mine, p)
            device = {'dm': self.mate}
        else:
            src = dst = shard.at(self.across, other, p)
            device = {'dm': self.mate}
        return remote(src, dst, self.send.at[k, hop], self.recv.at[k, hop], device)

    def arrival(self, k, hop):
        w, p = self.units[k]
        shard = self.shards[w]
        mine, other = self.row, 1 - self.row
        region = (shard.at(self.across, mine, p), shard.at(self.across, other, p), shard.at(self.cross, mine, p), shard.at(self.cross, other, p))[hop]
        return remote(region, region, self.send.at[k, hop], self.recv.at[k, hop], {'dm': self.mate})

    def own_copy(self, w, shard_index):
        shard = self.shards[w]
        return remote(shard.src, shard.whole(shard_index), self.own_send.at[w], self.own_recv.at[w], {'dm': self.mate})

    def start(self):
        for k in range(len(self.units)):
            self.copy(k, 0).start()
        for w in range(len(self.shards)):
            self.own_copy(w, self.me).start()

    def pass_y(self, k):
        self.arrival(k, 0).wait_recv()
        self.copy(k, 1).start()
        self.copy(k, 2).start()

    def pass_x(self, k):
        self.arrival(k, 1).wait_recv()
        self.copy(k, 3).start()

    def settle(self):
        for k in range(len(self.units)):
            self.arrival(k, 2).wait_recv()
            self.arrival(k, 3).wait_recv()
            for hop in range(4):
                self.copy(k, hop).wait_send()
        for w in range(len(self.shards)):
            self.own_copy(w, self.mate).wait_recv()
            self.own_copy(w, self.me).wait_send()


def fetch_kernel(x_ref, n_ref, wq_ref, wk_ref, wv_ref, wo_ref, xf_ref, nf_ref, wqf_ref, wkf_ref, wvf_ref, wof_ref, x_buf, n_buf, q_buf, k_buf, v_buf, o_buf, load_sem, store_sem, x_send, x_recv, n_send, n_recv, z_send, z_recv, own_send, own_recv, w_send, w_recv):
    row, line, me, mate, across, cross = places()
    seq = xf_ref.shape[0]
    part = seq // LINE
    cols = x_ref.shape[1]
    mine = pl.ds(pl.multiple_of(me * cols, cols), cols)
    shards = [Shard(wq_ref, wqf_ref, True, 1), Shard(wk_ref, wkf_ref, True, 1), Shard(wv_ref, wvf_ref, True, 1), Shard(wo_ref, wof_ref, False, 1)]
    gather = WeightGather(shards, own_send, own_recv, w_send, w_recv)

    def x_copy(hop):
        dev = (mate, across, cross)[hop]
        if hop == 0:
            src = x_ref.at[pl.ds(pl.multiple_of(dev * seq, seq), seq)]
            dst = xf_ref.at[:, mine]
        else:
            src = x_ref.at[pl.ds(pl.multiple_of(dev * seq + line * part, part), part)]
            dst = xf_ref.at[pl.ds(pl.multiple_of(line * part, part), part), mine]
        return remote(src, dst, x_send.at[hop], x_recv.at[hop], {'dm': dev})

    def x_arrival(hop):
        dev = (mate, across, cross)[hop]
        theirs = pl.ds(pl.multiple_of(dev * cols, cols), cols)
        if hop == 0:
            region = xf_ref.at[:, theirs]
        else:
            region = xf_ref.at[pl.ds(pl.multiple_of(line * part, part), part), theirs]
        return remote(region, region, x_send.at[hop], x_recv.at[hop], {'dm': dev})

    far = pl.ds(pl.multiple_of((1 - lax.div(me, 2)) * 2 * cols, 2 * cols), 2 * cols)

    def z_copy(up, block):
        region = xf_ref.at[pl.ds(pl.multiple_of(block * part, part), part), far]
        device = {'tp': line + 1} if up else {'tp': line - 1}
        return remote(region, region, z_send.at[0 if up else 1, block], z_recv.at[block], device)

    def z_step(step):
        below, above = line - step, line + step

        @pl.when(below >= 0)
        def _():
            z_copy(True, below).wait_recv()

            @pl.when(line < LINE - 1)
            def _():
                z_copy(True, below).start()

        @pl.when(above < LINE)
        def _():
            z_copy(False, above).wait_recv()

            @pl.when(line > 0)
            def _():
                z_copy(False, above).start()

    meet([{'dm': mate}, {'dm': across}, {'dm': cross}, {'dp': 1 - row}] + line_peers(line))
    x_copy(1).start()
    x_copy(2).start()
    x_copy(0).start()
    gather.start()
    n_copies = [remote(n_ref, nf_ref.at[me], n_send.at[i], n_recv.at[i], {'dm': dev}) for i, dev in enumerate((mate, across, cross))]
    n_arrivals = [remote(n_ref, nf_ref.at[dev], n_send.at[i], n_recv.at[i], {'dm': dev}) for i, dev in enumerate((mate, across, cross))]
    for copy in n_copies:
        copy.start()
    moves = [
        (x_ref.at[pl.ds(pl.multiple_of(me * seq, seq), seq)], x_buf, xf_ref.at[:, mine]),
        (wq_ref, q_buf, shards[0].whole(me)),
        (wk_ref, k_buf, shards[1].whole(me)),
        (wv_ref, v_buf, shards[2].whole(me)),
        (wo_ref, o_buf, shards[3].whole(me)),
        (n_ref, n_buf, nf_ref.at[me]),
    ]
    loads = [pltpu.make_async_copy(src, buf, load_sem.at[i]) for i, (src, buf, _) in enumerate(moves)]
    stores = [pltpu.make_async_copy(buf, dst, store_sem.at[i]) for i, (_, buf, dst) in enumerate(moves)]
    for load in loads:
        load.start()
    for load, store in zip(loads, stores):
        load.wait()
        store.start()

    x_arrival(1).wait_recv()
    x_arrival(2).wait_recv()

    @pl.when(line < LINE - 1)
    def _():
        z_copy(True, line).start()

    @pl.when(line > 0)
    def _():
        z_copy(False, line).start()

    z_step(1)
    gather.pass_y(0)
    gather.pass_y(1)
    z_step(2)
    gather.pass_y(2)
    gather.pass_x(0)
    gather.pass_x(1)
    z_step(3)
    gather.pass_y(3)
    gather.pass_x(2)
    gather.pass_x(3)
    gather.settle()
    x_arrival(0).wait_recv()
    for copy in n_arrivals:
        copy.wait_recv()
    for copy in n_copies:
        copy.wait_send()
    for hop in range(3):
        x_copy(hop).wait_send()
    for store in stores:
        store.wait()
    for block in range(LINE):

        @pl.when((block <= line) & (line < LINE - 1))
        def _():
            z_copy(True, block).wait_send()

        @pl.when((block >= line) & (line > 0))
        def _():
            z_copy(False, block).wait_send()


class LineSum:
    def __init__(self, p_ref, got, acc, out, sum_send, sum_recv, out_send, out_recv, finish, emit):
        self.p_ref, self.got, self.acc, self.out = p_ref, got, acc, out
        self.sum_send, self.sum_recv, self.out_send, self.out_recv = sum_send, sum_recv, out_send, out_recv
        self.finish, self.emit = finish, emit
        self.half = p_ref.shape[0] // 2
        self.chunks = self.half // CHUNK
        self.steps = self.chunks + 6 * LAG
        self.line = lax.axis_index('tp')

    def way(self, d):
        if d == 0:
            return self.line, {'tp': self.line + 1}, {'tp': self.line - 1}
        return LINE - 1 - self.line, {'tp': self.line - 1}, {'tp': self.line + 1}

    def rows(self, c):
        return pl.ds(pl.multiple_of(c * CHUNK, CHUNK), CHUNK)

    def out_rows(self, d, c):
        return pl.ds(pl.multiple_of(d * self.half + c * CHUNK, CHUNK), CHUNK)

    def sum_copy(self, d, c, first):
        src = self.p_ref.at[self.out_rows(d, c)] if first else self.acc.at[d, self.rows(c)]
        return remote(src, self.got.at[d, self.rows(c)], self.sum_send.at[d, c], self.sum_recv.at[d, c], self.way(d)[1])

    def out_copy(self, d, c):
        region = self.out.at[self.out_rows(d, c)]
        return remote(region, region, self.out_send.at[d, c], self.out_recv.at[d, c], self.way(d)[2])

    def step(self, t):
        for d in range(2):
            self.sum_step(d, t)
        for d in range(2):
            self.out_step(d, t)

    def sum_step(self, d, t):
        pos = self.way(d)[0]
        c = t - LAG * pos

        @pl.when((c >= 0) & (c < self.chunks))
        def _():
            @pl.when(pos == 0)
            def _():
                self.sum_copy(d, c, True).start()

            @pl.when(pos > 0)
            def _():
                self.sum_copy(d, c, False).wait_recv()
                total = self.p_ref[self.out_rows(d, c), :].astype(F32) + self.got[d, self.rows(c), :].astype(F32)

                @pl.when(pos < LINE - 1)
                def _():
                    self.acc[d, self.rows(c), :] = total.astype(BF16)
                    self.sum_copy(d, c, False).start()

                @pl.when(pos == LINE - 1)
                def _():
                    self.finish(self.out_rows(d, c), self.rows(c), total.astype(BF16))
                    self.out_copy(d, c).start()
                    self.emit(self.out_rows(d, c))

    def out_step(self, d, t):
        pos = self.way(d)[0]
        c = t - 3 * LAG - LAG * (LINE - 1 - pos)

        @pl.when((c >= 0) & (c < self.chunks) & (pos < LINE - 1))
        def _():
            self.out_copy(d, c).wait_recv()

            @pl.when(pos > 0)
            def _():
                self.out_copy(d, c).start()

            self.emit(self.out_rows(d, c))

    def run(self, actions):
        marks = sorted(set([0, self.steps] + [t for t in actions if 0 < t < self.steps]))
        for begin, end in zip(marks[:-1], marks[1:]):
            for action in actions.get(begin, ()):
                action()

            def body(t, carry):
                self.step(t)
                return carry

            lax.fori_loop(begin, end, body, 0)

    def settle(self):
        def body(c, carry):
            for d in range(2):
                pos = self.way(d)[0]

                @pl.when(pos < LINE - 1)
                def _():
                    self.sum_copy(d, c, False).wait_send()

                @pl.when(pos > 0)
                def _():
                    self.out_copy(d, c).wait_send()

            return carry

        lax.fori_loop(0, self.chunks, body, 0)


def unit_rows(values, gain):
    mean_sq = jnp.mean(values * values, axis=-1, keepdims=True)
    return values * lax.rsqrt(mean_sq + NORM_EPS) * gain


def middle_kernel(p_ref, xf_ref, n2_ref, n3_ref, wg_ref, wu_ref, wd_ref, m_ref, h_ref, wgf_ref, wuf_ref, wdf_ref, got, acc, m_buf, res_buf, row_buf, col_buf, res_sem, m_sem, h_sem, load_sem, store_sem, sum_send, sum_recv, out_send, out_recv, own_send, own_recv, w_send, w_recv):
    row, line, me, mate, across, cross = places()
    seq = p_ref.shape[0]
    half = seq // 2
    shards = [Shard(wg_ref, wgf_ref, True, 2), Shard(wu_ref, wuf_ref, True, 2), Shard(wd_ref, wdf_ref, False, 2)]
    gather = WeightGather(shards, own_send, own_recv, w_send, w_recv)
    first_row = pl.multiple_of(half * (1 - jnp.minimum(line, 1)), half)
    res_load = pltpu.make_async_copy(xf_ref.at[pl.ds(first_row, half)], res_buf, res_sem)
    h_store = pltpu.make_async_copy(res_buf, h_ref, h_sem)

    def finish(out_rows, rows, total):
        hidden = (res_buf[rows, :].astype(F32) + unit_rows(total.astype(F32), n2_ref[...])).astype(BF16)
        res_buf[rows, :] = hidden
        m_buf[out_rows, :] = unit_rows(hidden.astype(F32), n3_ref[...]).astype(BF16)

    def emit(out_rows):
        pltpu.make_async_copy(m_buf.at[out_rows], m_ref.at[out_rows], m_sem).start()

    sums = LineSum(p_ref, got, acc, m_buf, sum_send, sum_recv, out_send, out_recv, finish, emit)
    bufs = (row_buf, row_buf, col_buf)
    loads = [pltpu.make_async_copy(shard.src, buf, load_sem.at[w]) for w, (shard, buf) in enumerate(zip(shards, bufs))]
    stores = [pltpu.make_async_copy(buf, shard.whole(me), store_sem.at[w]) for w, (shard, buf) in enumerate(zip(shards, bufs))]

    meet([{'dm': mate}, {'dm': across}, {'dp': 1 - row}] + line_peers(line))
    res_load.start()
    loads[0].start()
    loads[2].start()
    gather.start()
    res_load.wait()

    def own_first():
        loads[0].wait()
        stores[0].start()
        loads[2].wait()
        stores[2].start()

    def own_second():
        stores[0].wait()
        loads[1].start()

    def own_third():
        loads[1].wait()
        stores[1].start()

    actions = {
        2: [own_first],
        5: [own_second],
        7: [own_third, functools.partial(gather.pass_y, 0)],
        13: [functools.partial(gather.pass_y, 1)],
        14: [functools.partial(gather.pass_x, 0)],
        18: [functools.partial(gather.pass_y, 2)],
        19: [functools.partial(gather.pass_x, 1)],
        23: [functools.partial(gather.pass_y, 3)],
        24: [functools.partial(gather.pass_x, 2)],
    }
    order = [action for t in sorted(actions) for action in actions[t]]
    sums.run({t: acts for t, acts in actions.items() if t < sums.steps})
    done = [action for t in sorted(actions) if t < sums.steps for action in actions[t]]
    for action in order[len(done):]:
        action()
    gather.pass_y(4)
    gather.pass_x(3)
    gather.pass_y(5)
    gather.pass_x(4)
    gather.pass_x(5)

    @pl.when((line == 0) | (line == LINE - 1))
    def _():
        h_store.start()
        h_store.wait()

    pltpu.make_async_copy(m_buf, m_ref, m_sem).wait()
    sums.settle()
    stores[1].wait()
    stores[2].wait()
    gather.settle()


def last_kernel(p_ref, h_ref, n4_ref, k_ref, v_ref, y_ref, kf_ref, vf_ref, got, acc, y_buf, res_buf, k_buf, v_buf, res_sem, kv_load, kv_store, kv_send, kv_recv, fin_send, fin_recv, own_sem, sum_send, sum_recv, out_send, out_recv):
    row, line, me, mate, across, cross = places()
    seq = p_ref.shape[0]
    cols = y_ref.shape[1]
    res_load = pltpu.make_async_copy(h_ref, res_buf, res_sem)
    ends = (line == 0) | (line == LINE - 1)
    caches = ((k_ref, kf_ref, k_buf), (v_ref, vf_ref, v_buf))

    def block(ref, shard):
        return ref.at[pl.ds(pl.multiple_of(shard * seq, seq), seq)]

    def kv_copy(i, hop):
        src, dst, _ = caches[i]
        if hop == 0:
            return remote(src, block(dst, me), kv_send.at[i, hop], kv_recv.at[i, hop], {'dm': across})
        if hop == 1:
            return remote(src, block(dst, me), kv_send.at[i, hop], kv_recv.at[i, hop], {'dm': mate})
        return remote(block(dst, across), block(dst, across), kv_send.at[i, hop], kv_recv.at[i, hop], {'dm': mate})

    def kv_arrival(i, hop):
        region = block(caches[i][1], (across, mate, cross)[hop])
        return remote(region, region, kv_send.at[i, hop], kv_recv.at[i, hop], {'dm': mate})

    kv_loads = [pltpu.make_async_copy(src, buf, kv_load.at[i]) for i, (src, _, buf) in enumerate(caches)]
    kv_stores = [pltpu.make_async_copy(buf, block(dst, me), kv_store.at[i]) for i, (_, dst, buf) in enumerate(caches)]

    def column(shard):
        return pl.ds(pl.multiple_of(shard * cols, cols), cols)

    def finish(out_rows, rows, total):
        y_buf[out_rows, :] = (res_buf[rows, :].astype(F32) + unit_rows(total.astype(F32), n4_ref[...])).astype(BF16)

    def emit(out_rows):
        start = out_rows.start
        there = pl.ds(pl.multiple_of(me * seq + start, CHUNK), CHUNK)
        for i, dev in enumerate((across, cross, mate)):
            remote(y_buf.at[out_rows, column(dev)], y_ref.at[there], fin_send.at[i], fin_recv.at[i], {'dm': dev}).start()
        pltpu.make_async_copy(y_buf.at[out_rows, column(me)], y_ref.at[there], own_sem).start()

    sums = LineSum(p_ref, got, acc, y_buf, sum_send, sum_recv, out_send, out_recv, finish, emit)

    meet([{'dm': mate}, {'dm': across}, {'dm': cross}] + line_peers(line))

    @pl.when(ends)
    def _():
        res_load.start()

    for i in range(2):
        kv_loads[i].start()
        kv_copy(i, 0).start()
        kv_copy(i, 1).start()

    @pl.when(ends)
    def _():
        res_load.wait()

    def keep_own():
        for i in range(2):
            kv_loads[i].wait()
            kv_stores[i].start()

    def pass_kv(i):
        kv_arrival(i, 0).wait_recv()
        kv_copy(i, 2).start()

    last = sums.steps - 1
    actions = {min(1, last): [keep_own], min(9, last): [functools.partial(pass_kv, 0), functools.partial(pass_kv, 1)]}
    if len(actions) == 1:
        actions = {last: [keep_own, functools.partial(pass_kv, 0), functools.partial(pass_kv, 1)]}
    sums.run(actions)
    sums.settle()
    for i in range(2):
        kv_stores[i].wait()
        for hop in range(3):
            kv_copy(i, hop).wait_send()
        kv_arrival(i, 1).wait_recv()
        kv_arrival(i, 2).wait_recv()
    for i, dev in enumerate((across, cross, mate)):
        done = remote(y_buf.at[:, column(dev)], block(y_ref, dev), fin_send.at[i], fin_recv.at[i], {'dm': dev})
        done.wait_send()
        done.wait_recv()
    pltpu.make_async_copy(y_buf.at[:, column(me)], block(y_ref, me), own_sem).wait()


def rotate(values, cos_tab, sin_tab):
    half_dim = values.shape[-1] // 2
    lower = values[:, :half_dim].astype(F32)
    upper = values[:, half_dim:].astype(F32)
    return jnp.concatenate([lower * cos_tab - upper * sin_tab, upper * cos_tab + lower * sin_tab], axis=-1).astype(BF16)


def attend_kernel(scale, q_ref, k_ref, v_ref, cos_ref, sin_ref, pos_col_ref, pos_row_ref, o_ref, k_out_ref, q_rot):
    seq = q_ref.shape[1]
    block = min(seq, 256)
    q_rot[...] = rotate(q_ref[0], cos_ref[...], sin_ref[...])
    k_out_ref[0] = rotate(k_ref[0], cos_ref[...], sin_ref[...])
    for i in range(seq // block):
        rows = slice(i * block, (i + 1) * block)
        span = (i + 1) * block
        scores = lax.dot_general(q_rot[rows, :], k_out_ref[0, :span, :], (((1,), (1,)), ((), ())), preferred_element_type=F32)
        capped = SOFT_CAP * jnp.tanh(scores * scale / SOFT_CAP)
        q_index = i * block + lax.broadcasted_iota(jnp.int32, (block, span), 0)
        key_index = lax.broadcasted_iota(jnp.int32, (block, span), 1)
        allowed = (key_index <= q_index) & (pos_col_ref[rows, :] - pos_row_ref[:, :span] < WINDOW_LEN)
        weights = jnp.where(allowed, jnp.exp(capped), 0.0)
        probs = (weights / jnp.sum(weights, axis=-1, keepdims=True)).astype(BF16)
        o_ref[rows, :] = jnp.dot(probs, v_ref[0, :span, :], preferred_element_type=F32).astype(BF16)


def gate_kernel(m_ref, wg_ref, wu_ref, z_ref):
    block = min(m_ref.shape[0], 512)

    def body(i, carry):
        rows = pl.ds(pl.multiple_of(i * block, block), block)
        gate = jnp.dot(m_ref[rows, :], wg_ref[...], preferred_element_type=F32).astype(BF16).astype(F32)
        up = jnp.dot(m_ref[rows, :], wu_ref[...], preferred_element_type=F32).astype(BF16).astype(F32)
        z_ref[rows, :] = (jax.nn.gelu(gate, approximate=True) * up).astype(BF16)
        return carry

    lax.fori_loop(0, m_ref.shape[0] // block, body, 0)


def like(*shape, dtype=BF16):
    return jax.ShapeDtypeStruct(shape, dtype)


def params(collective_id):
    return pltpu.CompilerParams(collective_id=collective_id, has_side_effects=True, vmem_limit_bytes=VMEM_BYTES)


def fetch(x, norms, wq, wk, wv, wo, seq):
    shard_rows, cols = wq.shape[0], x.shape[1]
    dim = 4 * cols
    return pl.pallas_call(
        fetch_kernel,
        name='fetch',
        out_shape=(like(seq, dim), like(4, *norms.shape), like(4 * shard_rows, *wq.shape[1:]), like(4 * shard_rows, *wk.shape[1:]), like(4 * shard_rows, *wv.shape[1:]), like(wo.shape[0], dim)),
        in_specs=[ANY] * 6,
        out_specs=(ANY,) * 6,
        scratch_shapes=[
            pltpu.VMEM((seq, cols), BF16), pltpu.VMEM(norms.shape, BF16), pltpu.VMEM(wq.shape, BF16), pltpu.VMEM(wk.shape, BF16), pltpu.VMEM(wv.shape, BF16), pltpu.VMEM(wo.shape, BF16),
            DMA((6,)), DMA((6,)), DMA((3,)), DMA((3,)), DMA((3,)), DMA((3,)), DMA((2, LINE)), DMA((LINE,)), DMA((4,)), DMA((4,)), DMA((4, 4)), DMA((4, 4)),
        ],
        compiler_params=params(0),
    )(x, norms, wq, wk, wv, wo)


def line_scratch(seq, dim):
    chunks = seq // 2 // CHUNK
    bufs = [pltpu.VMEM((2, seq // 2, dim), BF16), pltpu.VMEM((2, seq // 2, dim), BF16), pltpu.VMEM((seq, dim), BF16), pltpu.VMEM((seq // 2, dim), BF16)]
    return bufs, [DMA((2, chunks))] * 4


def middle(part, xf, gain2, gain3, wg, wu, wd):
    seq, dim = part.shape
    bufs, sems = line_scratch(seq, dim)
    return pl.pallas_call(
        middle_kernel,
        name='middle',
        out_shape=(like(seq, dim), like(seq // 2, dim), like(4 * wg.shape[0], wg.shape[1]), like(4 * wu.shape[0], wu.shape[1]), like(wd.shape[0], 4 * wd.shape[1])),
        in_specs=[VMEM, ANY, VMEM, VMEM, ANY, ANY, ANY],
        out_specs=(ANY,) * 5,
        scratch_shapes=bufs + [pltpu.VMEM(wg.shape, BF16), pltpu.VMEM(wd.shape, BF16), DMA, DMA, DMA, DMA((3,)), DMA((3,))] + sems + [DMA((3,)), DMA((3,)), DMA((6, 4)), DMA((6, 4))],
        compiler_params=params(1),
    )(part, xf, gain2, gain3, wg, wu, wd)


def last(part, hidden, gain4, k_own, v_own):
    seq, dim = part.shape
    bufs, sems = line_scratch(seq, dim)
    return pl.pallas_call(
        last_kernel,
        name='last',
        out_shape=(like(4 * seq, dim // 4), like(4 * seq, *k_own.shape[1:]), like(4 * seq, *v_own.shape[1:])),
        in_specs=[VMEM, ANY, VMEM, ANY, ANY],
        out_specs=(ANY,) * 3,
        scratch_shapes=bufs + [pltpu.VMEM(k_own.shape, BF16), pltpu.VMEM(v_own.shape, BF16), DMA, DMA((2,)), DMA((2,)), DMA((2, 3)), DMA((2, 3)), DMA((3,)), DMA((3,)), DMA] + sems,
        compiler_params=params(2),
    )(part, hidden, gain4, k_own, v_own)


def attend(q, k, v, cos_tab, sin_tab, pos, scale):
    heads, seq, head_dim = q.shape
    group = heads // k.shape[0]
    full = lambda shape: pl.BlockSpec(shape, lambda h: (0,) * len(shape))
    kv_spec = pl.BlockSpec((1, seq, head_dim), lambda h: (h // group, 0, 0))
    return pl.pallas_call(
        functools.partial(attend_kernel, scale),
        name='attend',
        grid=(heads,),
        out_shape=(like(seq, heads * head_dim), like(*k.shape)),
        in_specs=[pl.BlockSpec((1, seq, head_dim), lambda h: (h, 0, 0)), kv_spec, kv_spec, full(cos_tab.shape), full(sin_tab.shape), full((seq, 1)), full((1, seq))],
        out_specs=(pl.BlockSpec((seq, head_dim), lambda h: (0, h)), kv_spec),
        scratch_shapes=[pltpu.VMEM((seq, head_dim), BF16)],
        compiler_params=pltpu.CompilerParams(vmem_limit_bytes=VMEM_BYTES),
        cost_estimate=pl.CostEstimate(flops=4 * heads * seq * seq * head_dim, bytes_accessed=6 * heads * seq * head_dim, transcendentals=2 * heads * seq * seq),
    )(q, k, v, cos_tab, sin_tab, pos[:, None], pos[None, :])


def gate_up(m, wg, wu):
    seq, dim = m.shape
    hidden = wg.shape[1]
    tile = min(hidden, 512)
    w_spec = pl.BlockSpec((dim, tile), lambda f: (0, f))
    return pl.pallas_call(
        gate_kernel,
        name='gate_up',
        grid=(hidden // tile,),
        out_shape=like(seq, hidden),
        in_specs=[pl.BlockSpec((seq, dim), lambda f: (0, 0)), w_spec, w_spec],
        out_specs=pl.BlockSpec((seq, tile), lambda f: (0, f)),
        compiler_params=pltpu.CompilerParams(vmem_limit_bytes=VMEM_BYTES),
        cost_estimate=pl.CostEstimate(flops=4 * seq * dim * hidden, bytes_accessed=4 * dim * hidden, transcendentals=seq * hidden),
    )(m, wg, wu)


def solution(mesh):
    tp_size = mesh.shape['tp']

    def layer(tokens, positions, norm_pre_attn, w_query, w_key, w_value, w_out, norm_post_attn, norm_pre_ffw, w_gate, w_up, w_down, norm_post_ffw):
        seq = positions.shape[1]
        heads, head_dim, cols = w_out.shape
        dim = 4 * cols
        scale = (dim / (heads * tp_size)) ** -0.5
        norms = jnp.stack([norm_pre_attn, norm_post_attn, norm_pre_ffw, norm_post_ffw])
        xf, norms_all, wq, wk, wv, wo = fetch(tokens, norms, w_query, w_key, w_value, w_out.reshape(heads * head_dim, cols), seq)
        gains = 1.0 + jnp.swapaxes(norms_all, 0, 1).reshape(4, 1, dim).astype(F32)

        normed = lax.optimization_barrier(unit_rows(xf.astype(F32), gains[0]).astype(BF16))
        q, k, v = (jnp.einsum('nd,dhk->hnk', normed, w, preferred_element_type=F32).astype(BF16) for w in (wq, wk, wv))
        pos = lax.dynamic_index_in_dim(positions, lax.axis_index('dm'), 0, keepdims=False)
        half_dim = head_dim // 2
        inv_freq = ROPE_BASE ** (-2.0 * jnp.arange(half_dim, dtype=F32) / head_dim)
        angles = pos.astype(F32)[:, None] * inv_freq[None, :]
        attn_rows, k_rot = attend(q, k, v, jnp.cos(angles), jnp.sin(angles), pos, scale)

        attn_part = jnp.dot(attn_rows, wo, preferred_element_type=F32).astype(BF16)
        ffw_in, hidden, wg, wu, wd = middle(attn_part, xf, gains[1], gains[2], w_gate, w_up, w_down)
        gated = gate_up(ffw_in, wg, wu)
        down_part = jnp.dot(gated, wd, preferred_element_type=F32).astype(BF16)
        k_own, v_own = jnp.swapaxes(k_rot, 0, 1), jnp.swapaxes(v, 0, 1)
        return last(down_part, hidden, gains[3], k_own, v_own)

    width_spec = P('dm')
    in_specs = (P('dp', 'dm'), P('dp', None), width_spec, P('dm', 'tp', None), P('dm', 'tp', None), P('dm', 'tp', None), P('tp', None, 'dm'), width_spec, width_spec, P('dm', 'tp'), P('dm', 'tp'), P('tp', 'dm'), width_spec)
    out_specs = (P('dp', 'dm'), P('dp', 'tp', None), P('dp', 'tp', None))
    return jax.shard_map(layer, mesh=mesh, in_specs=in_specs, out_specs=out_specs, check_vma=False)
```

time: 2250 us -> 770 us (0.34)
  waiting for transfers between devices: 1700 us -> 0 us
  Pallas kernels: 0 us -> 666 us
  matrix products: 251 us -> 66 us
  other arithmetic: 158 us -> 15 us
  blocking collectives: 44.3 us -> 0 us
  local copies, waits for them, and re-layouts: 60.3 us -> 21.2 us
    psum x4 -> x0, waiting for transfers between devices: 1700 us -> none  [the longest x1 961 us: layer(): gate_proj, up_proj = lax.psum((gate_part, up_part), 'dm')]
    pallas_call x0 -> x5, Pallas kernels: none -> 666 us  [the longest x1 277 us: middle(): pl.pallas_call(middle_kernel, name='middle', out_shape=(like(seq, dim), l...]
    dot_general x15 -> x5, matrix products: 251 us -> 66 us  [the longest x1 32.9 us: layer(): down_part = jnp.dot(gated, wd, preferred_element_type=F32).astype(BF16)]
    sub x4 -> x0, other arithmetic: 91.8 us -> none  [one_block(): attn_probs = jax.nn.softmax(scores, axis=-1).astype(jnp.bfloat16)]
    psum x4 -> x0, blocking collectives: 44.3 us -> none  [norm_group(): sq_sum = lax.psum(jnp.sum(vals32 * vals32, axis=-1, keepdims=True), 'dm')]
    unnamed x38 -> x20, local copies, waits for them, and re-layouts: 43.4 us -> 13.5 us
  transfers between devices with their start and end apart: 4 -> 0, of which waited for: 4 -> 0; matrix products, arithmetic and copies ran while one was open for 2% -> 0% of each run, Pallas kernels for 0% -> 0%
where the time goes in v1:
time: 770 us; the launch traced here: 769 us
  Pallas kernels  666 us (86%)
  matrix products  66 us (9%)
  local copies, waits for them, and re-layouts  21.2 us (3%)
  other arithmetic  15 us (2%)
    pallas_call x1, Pallas kernels, middle(): pl.pallas_call(middle_kernel, name='middle', out_shape=(like(seq, dim), l...  277 us
    pallas_call x1, Pallas kernels, last(): pl.pallas_call(last_kernel, name='last', out_shape=(like(4 * seq, dim //...  201 us
    pallas_call x1, Pallas kernels, fetch(): pl.pallas_call(fetch_kernel, name='fetch', out_shape=(like(seq, dim), lik...  115 us
    pallas_call x1, Pallas kernels, gate_up(): pl.pallas_call(gate_kernel, name='gate_up', grid=(hidden // tile,), out_s...  62 us
    dot_general x1, matrix products, layer(): down_part = jnp.dot(gated, wd, preferred_element_type=F32).astype(BF16)  32.9 us
    dot_general x3, matrix products, layer(): jnp.einsum('nd,dhk->hnk', normed, w, preferred_element_type=F32)  20.3 us

profile of v1, /device:TPU:0, one launch (start us, length us, event | category | flops | bytes accessed | tf_op | source)
XLA Modules:
  0.0 769.1 jit_solution(10991355505847858006)
XLA Ops:
  0.6 0.7 stack.15
  1.3 0.7 stack.16
  2.0 0.7 stack.17
  2.7 0.7 stack.18
  3.4 0.6 pad_maximum_fusion.n_ref
  4.0 0.7 fusion.31
  4.7 0.0 copy-start.5
  4.7 1.0 copy.31.pos_col_ref
  5.8 3.1 multiply_sine_fusion
  8.8 115.3 %fetch.1 = (bf16[1024,3584]{1,0:T(8,128)(2,1)}, bf16[4,4,896]{2,1,0:T(4,128)(2,1)}, bf16[3584,4,256]{2,1,0:T(4,128)(2,1)}, bf16[3584,2,256]{2,1,0:T(2,128)(2,1)}...) custom-call(bf16[4096,896]{1,0:T(8,128)(2,1)} %x_ref.1, bf16[4,896]{1,0:T(4,128)(2,1)} %pad_maximum_fusion.n_ref, ...), custom_call_target="tpu_custom_call" | custom-call | tf_op jit(solution)/shard_map/fetch/pallas_call | solution.py:577
  124.1 0.0 copy-start.4
  124.1 4.6 fusion
  128.7 0.0 copy-done.5
  128.7 0.0 copy-done.4
  128.7 0.7 fusion.32
  129.4 6.0 fusion.2
  135.4 0.0 copy-start.7
  135.4 11.4 %convert_bitcast_fusion.q_ref = bf16[4,1024,256]{2,1,0:T(8,128)(2,1)} fusion(bf16[3584,4,256]{2,1,0:T(4,128)(2,1)} %get-tuple-element.16, bf16[1024,3584]{1,0:T(8,128)(2,1)S(1)} %fusion.2), kind=kOutput, calls=%fused_computation.16 | convolution fusion | flops 7517241344 | bytes 16777216 | tf_op jit(solution)/shard_map/nd,dhk->hnk/dot_general | solution.py:673
  146.8 0.0 copy-done.7
  146.8 0.0 copy-start.6
  146.8 4.1 fusion.16
  150.8 0.0 copy-done.6
  150.9 4.9 fusion.26.k_ref
  155.8 0.9 copy.35
  156.7 0.0 copy-start
  156.7 1.2 copy.30.v_ref
  157.9 10.8 %attend.1 = (bf16[1024,1024]{1,0:T(8,128)(2,1)}, bf16[2,1024,256]{2,1,0:T(8,128)(2,1)}) custom-call(bf16[4,1024,256]{2,1,0:T(8,128)(2,1)} %convert_bitcast_fusion.q_ref, bf16[2,1024,256]{2,1,0:T(8,128)(2,1)} %fusion.26.k_ref, bf16[2,1024,256]{2,1,0:T(8,128)(2,1)} %copy.30.v_ref, f32[1024,128]{1,0:T(8,128)} %get-tuple-element.36.cos_ref, ...), custom_call_target="tpu_custom_call" | custom-call | flops 4294967296 | bytes 6291456 | tf_op jit(solution)/shard_map/attend/pallas_call | solution.py:630
  168.7 0.0 copy-done
  168.7 0.0 copy-start.3
  168.8 12.8 %convolution_convert_fusion.p_ref = bf16[1024,3584]{1,0:T(8,128)(2,1)} fusion(bf16[1024,1024]{1,0:T(8,128)(2,1)} %get-tuple-element.21, bf16[1024,3584]{1,0:T(8,128)(2,1)} %get-tuple-element.22), kind=kOutput, calls=%fused_computation.5 | convolution fusion | flops 7519862784 | bytes 16777216 | tf_op jit(solution)/shard_map/dot_general | solution.py:680
  181.5 0.0 copy-done.3
  181.5 2.0 copy.51
  183.6 277.1 %middle.1 = (bf16[1024,3584]{1,0:T(8,128)(2,1)}, bf16[512,3584]{1,0:T(8,128)(2,1)}, bf16[3584,3584]{1,0:T(8,128)(2,1)}, bf16[3584,3584]{1,0:T(8,128)(2,1)}, bf16[3584,3584]{1,0:T(8,128)(2,1)}) custom-call(bf16[1024,3584]{1,0:T(8,128)(2,1)} %convolution_convert_fusion.p_ref, bf16[1024,3584]{1,0:T(8,128)(2,1)} %get-tuple-element.17.xf_ref, ...), custom_call_target="tpu_custom_call" | custom-call | tf_op jit(solution)/shard_map/middle/pallas_call | solution.py:600
  460.7 62.0 %gate_up.1 = bf16[1024,3584]{1,0:T(8,128)(2,1)} custom-call(bf16[1024,3584]{1,0:T(8,128)(2,1)} %get-tuple-element.23.m_ref, bf16[3584,3584]{1,0:T(8,128)(2,1)} %get-tuple-element.24.wg_ref, bf16[3584,3584]{1,0:T(8,128)(2,1)} %get-tuple-element.25.wu_ref), custom_call_target="tpu_custom_call" | custom-call | flops 52613349376 | bytes 51380224 | tf_op jit(solution)/shard_map/gate_up/pallas_call | solution.py:648
  522.7 32.9 %convolution_convert_fusion.1.p_ref = bf16[1024,3584]{1,0:T(8,128)(2,1)} fusion(bf16[1024,3584]{1,0:T(8,128)(2,1)} %gate_up.1, bf16[3584,3584]{1,0:T(8,128)(2,1)} %get-tuple-element.26), kind=kOutput, calls=%fused_computation.6 | convolution fusion | flops 26310344704 | bytes 40370176 | tf_op jit(solution)/shard_map/dot_general | solution.py:683
  555.7 200.8 %last.1 = (bf16[4096,896]{1,0:T(8,128)(2,1)}, bf16[4096,2,256]{2,1,0:T(2,128)(2,1)}, bf16[4096,2,256]{2,1,0:T(2,128)(2,1)}) custom-call(bf16[1024,3584]{1,0:T(8,128)(2,1)} %convolution_convert_fusion.1.p_ref, bf16[512,3584]{1,0:T(8,128)(2,1)} %get-tuple-element.27.h_ref, f32[1,3584]{1,0:T(1,128)} %bitcast.40, bf16[1024,2,256]{2,1,0:T(2,128)(2,1)} %bitcast.38, ...), custom_call_target="tpu_custom_call" | custom-call | tf_op jit(solution)/shard_map/last/pallas_call | solution.py:614
  756.5 0.0 copy-start.2
  756.5 6.9 copy.55
  763.4 0.0 copy-done.2
  763.4 0.0 copy-start.1
  763.4 2.1 copy.56
  765.6 1.6 copy-done.1
  767.1 2.0 copy.57
  (4 shorter events, 0.0 us)
Async XLA Ops:
  4.7 123.9 %copy-start.5 = (s32[1,1024]{1,0:T(1,128)}, s32[1,1024]{1,0:T(1,128)S(1)}, u32[]{:S(2)}) copy-start(s32[1,1024]{1,0:T(1,128)S(1)} %get-tuple-element.30.pos_row_ref) | copy-start | bytes 12292
  124.1 4.6 copy-start.4
  135.4 11.4 %copy-start.7 = (bf16[3584,2,256]{2,1,0:T(2,128)(2,1)S(1)}, bf16[3584,2,256]{2,1,0:T(2,128)(2,1)}, u32[]{:S(2)}) copy-start(bf16[3584,2,256]{2,1,0:T(2,128)(2,1)} %get-tuple-element.20) | copy-start | bytes 11010052
  146.8 4.1 copy-start.6
  156.7 12.0 %copy-start = (bf16[2,256,1024]{1,0,2:T(2,128)(2,1)}, bf16[2,256,1024]{1,0,2:T(2,128)(2,1)S(1)}, u32[]{:S(2)}) copy-start(bf16[2,256,1024]{1,0,2:T(2,128)(2,1)S(1)} %copy.35) | copy-start | bytes 3145732
  168.7 12.8 %copy-start.3 = (bf16[2,1024,256]{2,1,0:T(8,128)(2,1)S(1)}, bf16[2,1024,256]{2,1,0:T(8,128)(2,1)}, u32[]{:S(2)}) copy-start(bf16[2,1024,256]{2,1,0:T(8,128)(2,1)} %get-tuple-element.28) | copy-start | bytes 3145732
  756.5 6.9 copy-start.2
  763.4 3.7 copy-start.1

commit v2 on v1

v2 whole, which is shorter than its diff:
```python
import functools

import jax
import jax.numpy as jnp
from jax import lax
from jax.experimental import pallas as pl
from jax.experimental.pallas import tpu as pltpu
from jax.sharding import PartitionSpec as P

NORM_EPS = 1e-6
SOFT_CAP = 50.0
ROPE_BASE = 10000.0
WINDOW_LEN = 4096
BF16 = jnp.bfloat16
F32 = jnp.float32

CHUNK = 16
LAG = 2
LINE = 4
VMEM_BYTES = 62 * 1024 * 1024

ANY = pl.BlockSpec(memory_space=pl.ANY)
VMEM = pl.BlockSpec(memory_space=pltpu.VMEM)
DMA = pltpu.SemaphoreType.DMA


def places():
    row = lax.axis_index('dp')
    line = lax.axis_index('tp')
    me = lax.axis_index('dm')
    side = lax.div(me, 2)
    core = me - 2 * side
    return row, line, me, 2 * side + 1 - core, 2 * (1 - side) + core, 2 * (1 - side) + 1 - core


def remote(src, dst, send_sem, recv_sem, device):
    return pltpu.make_async_remote_copy(src_ref=src, dst_ref=dst, send_sem=send_sem, recv_sem=recv_sem, device_id=device, device_id_type=pl.DeviceIdType.MESH)


def meet(peers):
    barrier = pltpu.get_barrier_semaphore()
    for peer in peers:
        pl.semaphore_signal(barrier, inc=1, device_id=peer, device_id_type=pl.DeviceIdType.MESH)
    pl.semaphore_wait(barrier, len(peers))


def line_peers(line):
    return [{'tp': lax.rem(line + 1, LINE)}, {'tp': lax.rem(line + LINE - 1, LINE)}]


class Shard:
    def __init__(self, src, dst, by_rows, pieces):
        self.src, self.dst, self.by_rows, self.pieces = src, dst, by_rows, pieces
        self.rows = src.shape[0]
        self.unit = self.rows // (2 * pieces)

    def own(self, half, piece):
        return self.src.at[pl.ds(pl.multiple_of((half * self.pieces + piece) * self.unit, self.unit), self.unit)]

    def at(self, shard, half, piece):
        start = (half * self.pieces + piece) * self.unit
        if self.by_rows:
            return self.dst.at[pl.ds(pl.multiple_of(shard * self.rows + start, self.unit), self.unit)]
        cols = self.src.shape[1]
        return self.dst.at[pl.ds(pl.multiple_of(start, self.unit), self.unit), pl.ds(pl.multiple_of(shard * cols, cols), cols)]

    def whole(self, shard):
        if self.by_rows:
            return self.dst.at[pl.ds(pl.multiple_of(shard * self.rows, self.rows), self.rows)]
        cols = self.src.shape[1]
        return self.dst.at[:, pl.ds(pl.multiple_of(shard * cols, cols), cols)]


class WeightGather:
    def __init__(self, shards, own_send, own_recv, send, recv):
        self.shards, self.own_send, self.own_recv, self.send, self.recv = shards, own_send, own_recv, send, recv
        self.row, _, self.me, self.mate, self.across, self.cross = places()
        self.units = [(w, p) for w in range(len(shards)) for p in range(shards[w].pieces)]

    def copy(self, k, hop):
        w, p = self.units[k]
        shard = self.shards[w]
        mine, other = self.row, 1 - self.row
        if hop == 0:
            src, dst, device = shard.own(mine, p), shard.at(self.me, mine, p), {'dm': self.across}
        elif hop == 1:
            src = dst = shard.at(self.across, mine, p)
            device = {'dp': other}
        elif hop == 2:
            src = dst = shard.at(self.across, mine, p)
            device = {'dm': self.mate}
        else:
            src = dst = shard.at(self.across, other, p)
            device = {'dm': self.mate}
        return remote(src, dst, self.send.at[k, hop], self.recv.at[k, hop], device)

    def arrival(self, k, hop):
        w, p = self.units[k]
        shard = self.shards[w]
        mine, other = self.row, 1 - self.row
        region = (shard.at(self.across, mine, p), shard.at(self.across, other, p), shard.at(self.cross, mine, p), shard.at(self.cross, other, p))[hop]
        return remote(region, region, self.send.at[k, hop], self.recv.at[k, hop], {'dm': self.mate})

    def own_copy(self, w, shard_index):
        shard = self.shards[w]
        return remote(shard.src, shard.whole(shard_index), self.own_send.at[w], self.own_recv.at[w], {'dm': self.mate})

    def start(self):
        for k in range(len(self.units)):
            self.copy(k, 0).start()
        for w in range(len(self.shards)):
            self.own_copy(w, self.me).start()

    def pass_y(self, k):
        self.arrival(k, 0).wait_recv()
        self.copy(k, 1).start()
        self.copy(k, 2).start()

    def pass_x(self, k):
        self.arrival(k, 1).wait_recv()
        self.copy(k, 3).start()

    def settle_units(self, units, weights):
        for k in units:
            self.arrival(k, 2).wait_recv()
            self.arrival(k, 3).wait_recv()
            for hop in range(4):
                self.copy(k, hop).wait_send()
        for w in weights:
            self.own_copy(w, self.mate).wait_recv()
            self.own_copy(w, self.me).wait_send()


class LineSum:
    def __init__(self, p_buf, got, out, sum_send, sum_recv, out_send, out_recv, finish, emit):
        self.p_buf, self.got, self.out = p_buf, got, out
        self.sum_send, self.sum_recv, self.out_send, self.out_recv = sum_send, sum_recv, out_send, out_recv
        self.finish, self.emit = finish, emit
        self.half = p_buf.shape[0] // 2
        self.chunks = self.half // CHUNK
        self.steps = self.chunks + 6 * LAG
        self.line = lax.axis_index('tp')

    def way(self, d):
        if d == 0:
            return self.line, {'tp': self.line + 1}, {'tp': self.line - 1}
        return LINE - 1 - self.line, {'tp': self.line - 1}, {'tp': self.line + 1}

    def rows(self, c):
        return pl.ds(pl.multiple_of(c * CHUNK, CHUNK), CHUNK)

    def out_rows(self, d, c):
        return pl.ds(pl.multiple_of(d * self.half + c * CHUNK, CHUNK), CHUNK)

    def sum_copy(self, d, c):
        return remote(self.p_buf.at[self.out_rows(d, c)], self.got.at[d, self.rows(c)], self.sum_send.at[d, c], self.sum_recv.at[d, c], self.way(d)[1])

    def out_copy(self, d, c):
        region = self.out.at[self.out_rows(d, c)]
        return remote(region, region, self.out_send.at[d, c], self.out_recv.at[d, c], self.way(d)[2])

    def step(self, t):
        for d in range(2):
            self.sum_step(d, t)
        for d in range(2):
            self.out_step(d, t)

    def sum_step(self, d, t):
        pos = self.way(d)[0]
        c = t - LAG * pos

        @pl.when((c >= 0) & (c < self.chunks))
        def _():
            @pl.when(pos == 0)
            def _():
                self.sum_copy(d, c).start()

            @pl.when(pos > 0)
            def _():
                self.sum_copy(d, c).wait_recv()
                total = self.p_buf[self.out_rows(d, c), :].astype(F32) + self.got[d, self.rows(c), :].astype(F32)

                @pl.when(pos < LINE - 1)
                def _():
                    self.p_buf[self.out_rows(d, c), :] = total.astype(BF16)
                    self.sum_copy(d, c).start()

                @pl.when(pos == LINE - 1)
                def _():
                    self.finish(self.out_rows(d, c), self.rows(c), total.astype(BF16))
                    self.out_copy(d, c).start()
                    self.emit(self.out_rows(d, c))

    def out_step(self, d, t):
        pos = self.way(d)[0]
        c = t - 3 * LAG - LAG * (LINE - 1 - pos)

        @pl.when((c >= 0) & (c < self.chunks) & (pos < LINE - 1))
        def _():
            self.out_copy(d, c).wait_recv()

            @pl.when(pos > 0)
            def _():
                self.out_copy(d, c).start()

            self.emit(self.out_rows(d, c))

    def run(self, actions):
        def body(t, carry):
            for turn in sorted(actions):

                @pl.when(t == turn)
                def _():
                    for action in actions[turn]:
                        action()

            self.step(t)
            return carry

        lax.fori_loop(0, self.steps, body, 0)

    def settle(self):
        def body(c, carry):
            for d in range(2):
                pos = self.way(d)[0]

                @pl.when(pos < LINE - 1)
                def _():
                    self.sum_copy(d, c).wait_send()

                @pl.when(pos > 0)
                def _():
                    self.out_copy(d, c).wait_send()

            return carry

        lax.fori_loop(0, self.chunks, body, 0)


def unit_rows(values, gain):
    mean_sq = jnp.mean(values * values, axis=-1, keepdims=True)
    return values * lax.rsqrt(mean_sq + NORM_EPS) * gain


def rotate(values, cos_tab, sin_tab):
    half_dim = values.shape[-1] // 2
    lower = values[:, :half_dim].astype(F32)
    upper = values[:, half_dim:].astype(F32)
    return jnp.concatenate([lower * cos_tab - upper * sin_tab, upper * cos_tab + lower * sin_tab], axis=-1).astype(BF16)


def front_kernel(scale, kv_heads, head_dim, x_ref, n_ref, wqkv_ref, wo_ref, wg_ref, wu_ref, wd_ref, cos_ref, sin_ref, pos_col_ref, pos_row_ref, m_ref, h_ref, k_out_ref, v_out_ref, gain_ref, wgf_ref, wuf_ref, wdf_ref, xm_buf, w_buf, wo_buf, qkv_buf, o_buf, p_buf, got, res_buf, n_buf, x_send, x_recv, n_send, n_recv, z_send, z_recv, own_send, own_recv, w_send, w_recv, load_sem, keep_load, keep_store, m_sem, h_sem, kv_sem, sum_send, sum_recv, out_send, out_recv):
    row, line, me, mate, across, cross = places()
    seq, dim = xm_buf.shape
    cols = dim // 4
    half = seq // 2
    quarter = seq // LINE
    sub = quarter // 2
    heads = wo_ref.shape[0] // head_dim
    group = heads // kv_heads
    mine = pl.ds(pl.multiple_of(me * cols, cols), cols)
    shards = [Shard(wqkv_ref, w_buf, True, 4), Shard(wo_ref, wo_buf, False, 2), Shard(wg_ref, wgf_ref, True, 4), Shard(wu_ref, wuf_ref, True, 4), Shard(wd_ref, wdf_ref, False, 4)]
    gather = WeightGather(shards, own_send, own_recv, w_send, w_recv)
    first, out_first, ffw_first, units = 0, 4, 6, 18
    peers = (mate, across, cross)

    def x_copy(hop, s):
        dev = peers[hop]
        if hop == 0:
            src, dst = x_ref.at[pl.ds(pl.multiple_of(dev * seq, seq), seq)], xm_buf.at[:, mine]
        else:
            start = line * quarter + s * sub
            src = x_ref.at[pl.ds(pl.multiple_of(dev * seq + start, sub), sub)]
            dst = xm_buf.at[pl.ds(pl.multiple_of(start, sub), sub), mine]
        return remote(src, dst, x_send.at[hop, s], x_recv.at[hop, s], {'dm': dev})

    def x_arrival(hop, s):
        dev = peers[hop]
        theirs = pl.ds(pl.multiple_of(dev * cols, cols), cols)
        region = xm_buf.at[:, theirs] if hop == 0 else xm_buf.at[pl.ds(pl.multiple_of(line * quarter + s * sub, sub), sub), theirs]
        return remote(region, region, x_send.at[hop, s], x_recv.at[hop, s], {'dm': dev})

    far = pl.ds(pl.multiple_of((1 - lax.div(me, 2)) * 2 * cols, 2 * cols), 2 * cols)

    def z_copy(up, block, s):
        index = 2 * block + s
        region = xm_buf.at[pl.ds(pl.multiple_of(index * sub, sub), sub), far]
        device = {'tp': line + 1} if up else {'tp': line - 1}
        return remote(region, region, z_send.at[0 if up else 1, index], z_recv.at[index], device)

    def z_first(s):
        x_arrival(1, s).wait_recv()
        x_arrival(2, s).wait_recv()

        @pl.when(line < LINE - 1)
        def _():
            z_copy(True, line, s).start()

        @pl.when(line > 0)
        def _():
            z_copy(False, line, s).start()

    def z_step(step, s):
        below, above = line - step, line + step

        @pl.when(below >= 0)
        def _():
            z_copy(True, below, s).wait_recv()

            @pl.when(line < LINE - 1)
            def _():
                z_copy(True, below, s).start()

        @pl.when(above < LINE)
        def _():
            z_copy(False, above, s).wait_recv()

            @pl.when(line > 0)
            def _():
                z_copy(False, above, s).start()

    n_copies = [remote(n_ref, n_buf.at[me], n_send.at[i], n_recv.at[i], {'dm': dev}) for i, dev in enumerate(peers)]
    n_arrivals = [remote(n_ref, n_buf.at[dev], n_send.at[i], n_recv.at[i], {'dm': dev}) for i, dev in enumerate(peers)]
    loads = [
        pltpu.make_async_copy(x_ref.at[pl.ds(pl.multiple_of(me * seq, seq), seq)], xm_buf.at[:, mine], load_sem.at[0]),
        pltpu.make_async_copy(wqkv_ref, shards[0].whole(me), load_sem.at[1]),
        pltpu.make_async_copy(wo_ref, shards[1].whole(me), load_sem.at[2]),
        pltpu.make_async_copy(n_ref, n_buf.at[me], load_sem.at[3]),
    ]
    rows = wg_ref.shape[0]
    down_rows = wd_ref.shape[0] // 4
    keeps = []
    for w in (2, 3):
        keeps.append([(shards[w].src, p_buf.at[:rows], shards[w].whole(me))])
    keeps.append([(wd_ref.at[pl.ds(i * down_rows, down_rows)], p_buf.at[:down_rows, pl.ds(i * cols, cols)], wdf_ref.at[pl.ds(i * down_rows, down_rows), mine]) for i in range(4)])

    def keep(i, storing):
        moves = keeps[i]
        return [pltpu.make_async_copy(buf, dst, keep_store.at[n]) if storing else pltpu.make_async_copy(src, buf, keep_load.at[n]) for n, (src, buf, dst) in enumerate(moves)]

    def keep_load_start(i):
        for copy in keep(i, False):
            copy.start()

    def keep_store_start(i):
        for copy in keep(i, False):
            copy.wait()
        for copy in keep(i, True):
            copy.start()

    def keep_done(i):
        for copy in keep(i, True):
            copy.wait()

    meet([{'dm': mate}, {'dm': across}, {'dm': cross}, {'dp': 1 - row}] + line_peers(line))
    for s in range(2):
        x_copy(1, s).start()
        x_copy(2, s).start()
    x_copy(0, 0).start()
    for copy in n_copies:
        copy.start()
    gather.start()
    for load in loads:
        load.start()
    keep_load_start(0)
    z_first(0)
    keep_store_start(0)
    z_first(1)
    keep_done(0)
    keep_load_start(1)
    z_step(1, 0)
    gather.pass_y(0)
    keep_store_start(1)
    z_step(1, 1)
    gather.pass_y(1)
    keep_done(1)
    keep_load_start(2)
    z_step(2, 0)
    gather.pass_x(0)
    gather.pass_y(2)
    keep_store_start(2)
    z_step(2, 1)
    gather.pass_x(1)
    gather.pass_y(3)
    z_step(3, 0)
    gather.pass_x(2)
    for copy in n_arrivals:
        copy.wait_recv()
    for load in loads:
        load.wait()
    for shard in range(4):
        gain_ref[:, shard * cols:(shard + 1) * cols] = 1.0 + n_buf[shard]
    x_arrival(0, 0).wait_recv()
    z_step(3, 1)
    gather.pass_x(3)

    for block in range(LINE):
        for s in range(2):

            @pl.when((block <= line) & (line < LINE - 1))
            def _():
                z_copy(True, block, s).wait_send()

            @pl.when((block >= line) & (line > 0))
            def _():
                z_copy(False, block, s).wait_send()

    first_row = pl.multiple_of(half * (1 - jnp.minimum(line, 1)), half)
    res_buf[...] = xm_buf[pl.ds(first_row, half), :]
    norm_rows = min(seq, 64)

    def norm_body(i, carry):
        part = pl.ds(pl.multiple_of(i * norm_rows, norm_rows), norm_rows)
        xm_buf[part, :] = unit_rows(xm_buf[part, :].astype(F32), gain_ref[0:1, :]).astype(BF16)
        return carry

    lax.fori_loop(0, seq // norm_rows, norm_body, 0)
    gather.settle_units(range(0, 4), [0])
    gather.pass_y(4)
    gather.pass_y(5)
    keep_done(2)

    big = min(seq, 512)
    width = qkv_buf.shape[1]
    tile = min(width, 512)

    def qkv_body(i, carry):
        column = pl.ds(pl.multiple_of(lax.rem(i, width // tile) * tile, tile), tile)
        part = pl.ds(pl.multiple_of(lax.div(i, width // tile) * big, big), big)
        qkv_buf[part, column] = jnp.dot(xm_buf[part, :], w_buf[:, column], preferred_element_type=F32).astype(BF16)
        return carry

    lax.fori_loop(0, (width // tile) * (seq // big), qkv_body, 0)
    gather.pass_x(4)
    gather.pass_x(5)
    gather.pass_y(6)

    def rotate_body(i, carry):
        column = pl.ds(pl.multiple_of(i * head_dim, head_dim), head_dim)
        qkv_buf[:, column] = rotate(qkv_buf[:, column], cos_ref[...], sin_ref[...])
        return carry

    lax.fori_loop(0, heads + kv_heads, rotate_body, 0)
    kv_copies = []
    for i in range(kv_heads):
        for n, ref in enumerate((k_out_ref, v_out_ref)):
            start = (heads + n * kv_heads + i) * head_dim
            kv_copies.append(pltpu.make_async_copy(qkv_buf.at[:, pl.ds(start, head_dim)], ref.at[i], kv_sem.at[n, i]))
    for copy in kv_copies:
        copy.start()

    block = seq // 8
    d_tile = min(dim, 512)

    def attend_block(i):
        part = slice(i * block, (i + 1) * block)
        span = (i + 1) * block
        q_index = i * block + lax.broadcasted_iota(jnp.int32, (block, span), 0)
        key_index = lax.broadcasted_iota(jnp.int32, (block, span), 1)
        allowed = (key_index <= q_index) & (pos_col_ref[part, :] - pos_row_ref[:, :span] < WINDOW_LEN)

        def head_body(h, carry):
            q_cols = pl.ds(pl.multiple_of(h * head_dim, head_dim), head_dim)
            k_cols = pl.ds(pl.multiple_of((heads + lax.div(h, group)) * head_dim, head_dim), head_dim)
            v_cols = pl.ds(pl.multiple_of((heads + kv_heads + lax.div(h, group)) * head_dim, head_dim), head_dim)
            scores = lax.dot_general(qkv_buf[part, q_cols], qkv_buf[:span, k_cols], (((1,), (1,)), ((), ())), preferred_element_type=F32)
            capped = SOFT_CAP * jnp.tanh(scores * scale / SOFT_CAP)
            weights = jnp.where(allowed, jnp.exp(capped), 0.0)
            probs = (weights / jnp.sum(weights, axis=-1, keepdims=True)).astype(BF16)
            o_buf[part, q_cols] = jnp.dot(probs, qkv_buf[:span, v_cols], preferred_element_type=F32).astype(BF16)
            return carry

        lax.fori_loop(0, heads, head_body, 0)

    def out_block(i):
        part = slice(i * block, (i + 1) * block)

        def out_body(n, carry):
            column = pl.ds(pl.multiple_of(n * d_tile, d_tile), d_tile)
            p_buf[part, column] = jnp.dot(o_buf[part, :], wo_buf[:, column], preferred_element_type=F32).astype(BF16)
            return carry

        lax.fori_loop(0, dim // d_tile, out_body, 0)

    attend_block(0)
    attend_block(4)
    gather.settle_units(range(4, 6), [1])
    out_block(0)
    out_block(4)
    gather.pass_y(7)

    def finish(out_rows, rows, total):
        hidden = (res_buf[rows, :].astype(F32) + unit_rows(total.astype(F32), gain_ref[1:2, :])).astype(BF16)
        res_buf[rows, :] = hidden
        xm_buf[out_rows, :] = unit_rows(hidden.astype(F32), gain_ref[2:3, :]).astype(BF16)

    def emit(out_rows):
        pltpu.make_async_copy(xm_buf.at[out_rows], m_ref.at[out_rows], m_sem).start()

    sums = LineSum(p_buf, got, xm_buf, sum_send, sum_recv, out_send, out_recv, finish, emit)

    ahead = block // CHUNK
    actions = {}

    def at(t, action):
        actions.setdefault(min(max(t, 0), sums.steps - 1), []).append(action)

    def both(i):
        attend_block(i)
        out_block(i)

    for i in range(1, 4):
        at(i * ahead - (5 * ahead) // 8, functools.partial(both, i))
        at(i * ahead - (3 * ahead) // 8, functools.partial(both, 4 + i))
    turn = sums.steps / 44.0
    y_turns = (8, 11, 15, 18, 22, 25, 29, 32, 36, 41)
    for k in range(8, units):
        at(int(y_turns[k - 8] * turn), functools.partial(gather.pass_y, k))
    x_turns = (4, 9, 12, 16, 19, 23, 26, 30, 33, 38, 43)
    for k in range(6, units - 1):
        at(int(x_turns[k - 6] * turn), functools.partial(gather.pass_x, k))
    sums.run(actions)
    gather.pass_x(units - 1)

    h_store = pltpu.make_async_copy(res_buf, h_ref, h_sem)
    ends = (line == 0) | (line == LINE - 1)

    @pl.when(ends)
    def _():
        h_store.start()

    pltpu.make_async_copy(xm_buf, m_ref, m_sem).wait()
    sums.settle()
    gather.settle_units(range(6, units), [2, 3, 4])
    for copy in kv_copies:
        copy.wait()
    for copy in n_copies:
        copy.wait_send()
    x_copy(0, 0).wait_send()
    for s in range(2):
        x_copy(1, s).wait_send()
        x_copy(2, s).wait_send()

    @pl.when(ends)
    def _():
        h_store.wait()


def last_kernel(p_ref, h_ref, n4_ref, k_ref, v_ref, y_ref, kf_ref, vf_ref, p_buf, got, y_buf, res_buf, k_buf, v_buf, res_sem, kv_load, kv_store, kv_send, kv_recv, fin_send, fin_recv, own_sem, p_sem, sum_send, sum_recv, out_send, out_recv):
    row, line, me, mate, across, cross = places()
    seq = p_ref.shape[0]
    cols = y_ref.shape[1]
    res_load = pltpu.make_async_copy(h_ref, res_buf, res_sem)
    p_load = pltpu.make_async_copy(p_ref, p_buf, p_sem)
    ends = (line == 0) | (line == LINE - 1)
    caches = ((k_ref, kf_ref, k_buf), (v_ref, vf_ref, v_buf))

    def block(ref, shard):
        return ref.at[pl.ds(pl.multiple_of(shard * seq, seq), seq)]

    def kv_copy(i, hop):
        src, dst, _ = caches[i]
        if hop == 0:
            return remote(src, block(dst, me), kv_send.at[i, hop], kv_recv.at[i, hop], {'dm': across})
        if hop == 1:
            return remote(src, block(dst, me), kv_send.at[i, hop], kv_recv.at[i, hop], {'dm': mate})
        return remote(block(dst, across), block(dst, across), kv_send.at[i, hop], kv_recv.at[i, hop], {'dm': mate})

    def kv_arrival(i, hop):
        region = block(caches[i][1], (across, mate, cross)[hop])
        return remote(region, region, kv_send.at[i, hop], kv_recv.at[i, hop], {'dm': mate})

    kv_loads = [pltpu.make_async_copy(src, buf, kv_load.at[i]) for i, (src, _, buf) in enumerate(caches)]
    kv_stores = [pltpu.make_async_copy(buf, block(dst, me), kv_store.at[i]) for i, (_, dst, buf) in enumerate(caches)]

    def column(shard):
        return pl.ds(pl.multiple_of(shard * cols, cols), cols)

    def finish(out_rows, rows, total):
        y_buf[out_rows, :] = (res_buf[rows, :].astype(F32) + unit_rows(total.astype(F32), n4_ref[3:4, :])).astype(BF16)

    def emit(out_rows):
        start = out_rows.start
        there = pl.ds(pl.multiple_of(me * seq + start, CHUNK), CHUNK)
        for i, dev in enumerate((across, cross, mate)):
            remote(y_buf.at[out_rows, column(dev)], y_ref.at[there], fin_send.at[i], fin_recv.at[i], {'dm': dev}).start()
        pltpu.make_async_copy(y_buf.at[out_rows, column(me)], y_ref.at[there], own_sem).start()

    sums = LineSum(p_buf, got, y_buf, sum_send, sum_recv, out_send, out_recv, finish, emit)

    p_load.start()
    meet([{'dm': mate}, {'dm': across}, {'dm': cross}] + line_peers(line))

    @pl.when(ends)
    def _():
        res_load.start()

    for i in range(2):
        kv_loads[i].start()
        kv_copy(i, 0).start()
        kv_copy(i, 1).start()

    @pl.when(ends)
    def _():
        res_load.wait()

    p_load.wait()

    def keep_own():
        for i in range(2):
            kv_loads[i].wait()
            kv_stores[i].start()

    def pass_kv(i):
        kv_arrival(i, 0).wait_recv()
        kv_copy(i, 2).start()

    actions = {1: [keep_own], min(14, sums.steps - 2): [functools.partial(pass_kv, 0)], min(17, sums.steps - 1): [functools.partial(pass_kv, 1)]}
    sums.run(actions)
    sums.settle()
    for i in range(2):
        kv_stores[i].wait()
        for hop in range(3):
            kv_copy(i, hop).wait_send()
        kv_arrival(i, 1).wait_recv()
        kv_arrival(i, 2).wait_recv()
    for i, dev in enumerate((across, cross, mate)):
        done = remote(y_buf.at[:, column(dev)], block(y_ref, dev), fin_send.at[i], fin_recv.at[i], {'dm': dev})
        done.wait_send()
        done.wait_recv()
    pltpu.make_async_copy(y_buf.at[:, column(me)], block(y_ref, me), own_sem).wait()


def gate_kernel(m_ref, wg_ref, wu_ref, z_ref):
    block = min(m_ref.shape[0], 512)

    def body(i, carry):
        rows = pl.ds(pl.multiple_of(i * block, block), block)
        gate = jnp.dot(m_ref[rows, :], wg_ref[...], preferred_element_type=F32).astype(BF16).astype(F32)
        up = jnp.dot(m_ref[rows, :], wu_ref[...], preferred_element_type=F32).astype(BF16).astype(F32)
        z_ref[rows, :] = (jax.nn.gelu(gate, approximate=True) * up).astype(BF16)
        return carry

    lax.fori_loop(0, m_ref.shape[0] // block, body, 0)


def like(*shape, dtype=BF16):
    return jax.ShapeDtypeStruct(shape, dtype)


def params(collective_id):
    return pltpu.CompilerParams(collective_id=collective_id, has_side_effects=True, vmem_limit_bytes=VMEM_BYTES)


def line_scratch(seq, dim):
    chunks = seq // 2 // CHUNK
    return [DMA((2, chunks))] * 4


def front(x, norms, wqkv, wo, wg, wu, wd, cos_tab, sin_tab, pos, scale, kv_heads, head_dim):
    seq = pos.shape[0]
    cols = x.shape[1]
    dim = 4 * cols
    width = wqkv.shape[1]
    units = 18
    return pl.pallas_call(
        functools.partial(front_kernel, scale, kv_heads, head_dim),
        name='front',
        out_shape=(like(seq, dim), like(seq // 2, dim), like(kv_heads, seq, head_dim), like(kv_heads, seq, head_dim), like(8, dim, dtype=F32), like(4 * wg.shape[0], wg.shape[1]), like(4 * wu.shape[0], wu.shape[1]), like(wd.shape[0], 4 * wd.shape[1])),
        in_specs=[ANY] * 7 + [VMEM] * 4,
        out_specs=(ANY,) * 4 + (VMEM,) + (ANY,) * 3,
        scratch_shapes=[
            pltpu.VMEM((seq, dim), BF16), pltpu.VMEM((dim, width), BF16), pltpu.VMEM((wo.shape[0], dim), BF16), pltpu.VMEM((seq, width), BF16), pltpu.VMEM((seq, wo.shape[0]), BF16),
            pltpu.VMEM((seq, dim), BF16), pltpu.VMEM((2, seq // 2, dim), BF16), pltpu.VMEM((seq // 2, dim), BF16), pltpu.VMEM((4,) + norms.shape, F32),
            DMA((3, 2)), DMA((3, 2)), DMA((3,)), DMA((3,)), DMA((2, 2 * LINE)), DMA((2 * LINE,)), DMA((5,)), DMA((5,)), DMA((units, 4)), DMA((units, 4)), DMA((4,)), DMA((4,)), DMA((4,)), DMA, DMA, DMA((2, kv_heads)),
        ] + line_scratch(seq, dim),
        compiler_params=params(0),
    )(x, norms, wqkv, wo, wg, wu, wd, cos_tab, sin_tab, pos[:, None], pos[None, :])


def last(part, hidden, gains, k_own, v_own):
    seq, dim = part.shape
    return pl.pallas_call(
        last_kernel,
        name='last',
        out_shape=(like(4 * seq, dim // 4), like(4 * seq, *k_own.shape[1:]), like(4 * seq, *v_own.shape[1:])),
        in_specs=[ANY, ANY, VMEM, ANY, ANY],
        out_specs=(ANY,) * 3,
        scratch_shapes=[pltpu.VMEM((seq, dim), BF16), pltpu.VMEM((2, seq // 2, dim), BF16), pltpu.VMEM((seq, dim), BF16), pltpu.VMEM((seq // 2, dim), BF16), pltpu.VMEM(k_own.shape, BF16), pltpu.VMEM(v_own.shape, BF16), DMA, DMA((2,)), DMA((2,)), DMA((2, 3)), DMA((2, 3)), DMA((3,)), DMA((3,)), DMA, DMA] + line_scratch(seq, dim),
        compiler_params=params(2),
    )(part, hidden, gains, k_own, v_own)


def gate_up(m, wg, wu):
    seq, dim = m.shape
    hidden = wg.shape[1]
    tile = min(hidden, 512)
    w_spec = pl.BlockSpec((dim, tile), lambda f: (0, f))
    return pl.pallas_call(
        gate_kernel,
        name='gate_up',
        grid=(hidden // tile,),
        out_shape=like(seq, hidden),
        in_specs=[pl.BlockSpec((seq, dim), lambda f: (0, 0)), w_spec, w_spec],
        out_specs=pl.BlockSpec((seq, tile), lambda f: (0, f)),
        compiler_params=pltpu.CompilerParams(vmem_limit_bytes=VMEM_BYTES),
        cost_estimate=pl.CostEstimate(flops=4 * seq * dim * hidden, bytes_accessed=4 * dim * hidden, transcendentals=seq * hidden),
    )(m, wg, wu)


def solution(mesh):
    tp_size = mesh.shape['tp']

    def layer(tokens, positions, norm_pre_attn, w_query, w_key, w_value, w_out, norm_post_attn, norm_pre_ffw, w_gate, w_up, w_down, norm_post_ffw):
        seq = positions.shape[1]
        heads, head_dim, cols = w_out.shape
        dim = 4 * cols
        scale = (dim / (heads * tp_size)) ** -0.5
        norms = jnp.stack([norm_pre_attn, norm_post_attn, norm_pre_ffw, norm_post_ffw]).astype(F32)
        norms = jnp.concatenate([norms, jnp.zeros_like(norms)])
        wqkv = jnp.concatenate([w.reshape(w.shape[0], -1) for w in (w_query, w_key, w_value)], axis=1)
        pos = lax.dynamic_index_in_dim(positions, lax.axis_index('dm'), 0, keepdims=False)
        half_dim = head_dim // 2
        inv_freq = ROPE_BASE ** (-2.0 * jnp.arange(half_dim, dtype=F32) / head_dim)
        angles = pos.astype(F32)[:, None] * inv_freq[None, :]
        ffw_in, hidden, k_rot, v, gains, wg, wu, wd = front(tokens, norms, wqkv, w_out.reshape(heads * head_dim, cols), w_gate, w_up, w_down, jnp.cos(angles), jnp.sin(angles), pos, scale, w_key.shape[1], head_dim)
        gated = gate_up(ffw_in, wg, wu)
        down_part = jnp.dot(gated, wd, preferred_element_type=F32).astype(BF16)
        k_own, v_own = jnp.swapaxes(k_rot, 0, 1), jnp.swapaxes(v, 0, 1)
        return last(down_part, hidden, gains, k_own, v_own)

    width_spec = P('dm')
    in_specs = (P('dp', 'dm'), P('dp', None), width_spec, P('dm', 'tp', None), P('dm', 'tp', None), P('dm', 'tp', None), P('tp', None, 'dm'), width_spec, width_spec, P('dm', 'tp'), P('dm', 'tp'), P('tp', 'dm'), width_spec)
    out_specs = (P('dp', 'dm'), P('dp', 'tp', None), P('dp', 'tp', None))
    return jax.shard_map(layer, mesh=mesh, in_specs=in_specs, out_specs=out_specs, check_vma=False)
```

time: 770 us -> 638 us (0.83)
  Pallas kernels: 666 us -> 566 us
  matrix products: 66 us -> 33.1 us
  local copies, waits for them, and re-layouts: 21.2 us -> 30.8 us
  other arithmetic: 15 us -> 6.49 us
    pallas_call x3 -> x1, Pallas kernels: 403 us -> 321 us  [front(): pl.pallas_call(functools.partial(front_kernel, scale, kv_heads, head_dim)...]
    dot_general x4 -> x0, matrix products: 33.1 us -> none  [the longest x3 20.3 us: layer(): jnp.einsum('nd,dhk->hnk', normed, w, preferred_element_type=F32)]
    pallas_call x1, Pallas kernels: 201 us -> 184 us  [last(): pl.pallas_call(last_kernel, name='last', out_shape=(like(4 * seq, dim //...]
    transpose x0 -> x1, local copies, waits for them, and re-layouts: none -> 9.79 us  [layer(): k_own, v_own = (jnp.swapaxes(k_rot, 0, 1), jnp.swapaxes(v, 0, 1))]
    unnamed x20 -> x16, local copies, waits for them, and re-layouts: 13.5 us -> 17.3 us
where the time goes in v2:
time: 638 us
  Pallas kernels  566 us (89%)
  matrix products  33.1 us (5%)
  local copies, waits for them, and re-layouts  30.8 us (5%)
  other arithmetic  6.49 us (1%)
    pallas_call x1, Pallas kernels, front(): pl.pallas_call(functools.partial(front_kernel, scale, kv_heads, head_dim)...  321 us
    pallas_call x1, Pallas kernels, last(): pl.pallas_call(last_kernel, name='last', out_shape=(like(4 * seq, dim //...  184 us
    pallas_call x1, Pallas kernels, gate_up(): pl.pallas_call(gate_kernel, name='gate_up', grid=(hidden // tile,), out_s...  62 us
    dot_general x1, matrix products, layer(): down_part = jnp.dot(gated, wd, preferred_element_type=F32).astype(BF16)  33.1 us
    unnamed x16, local copies, waits for them, and re-layouts  17.3 us

profile of v2, /device:TPU:0, one launch (start us, length us, event | category | flops | bytes accessed | tf_op | source)
XLA Modules:
  0.0 637.5 jit_solution(1060053636419688676)
XLA Ops:
  0.6 0.7 stack.15
  1.3 0.7 stack.16
  2.0 0.7 stack.17
  2.7 0.7 stack.18
  3.4 0.7 fusion.8
  4.1 0.0 copy-start.4
  4.1 0.6 fusion.7.n_ref
  4.8 1.0 copy.18.pos_col_ref
  5.8 1.4 copy.22
  7.2 1.4 copy.23
  8.6 3.1 multiply_sine_fusion
  11.6 1.9 copy.21
  13.5 2.1 pad_maximum_fusion.wqkv_ref
  15.6 0.0 copy-done.4
  15.6 320.8 %front.1 = (bf16[1024,3584]{1,0:T(8,128)(2,1)}, bf16[512,3584]{1,0:T(8,128)(2,1)}, bf16[2,1024,256]{2,1,0:T(8,128)(2,1)}, bf16[2,1024,256]{2,1,0:T(8,128)(2,1)},...) custom-call(bf16[4096,896]{1,0:T(8,128)(2,1)} %x_ref.1, ...), custom_call_target="tpu_custom_call" | custom-call | tf_op jit(solution)/shard_map/front/pallas_call | solution.py:666
  336.4 62.0 %gate_up.1 = bf16[1024,3584]{1,0:T(8,128)(2,1)} custom-call(bf16[1024,3584]{1,0:T(8,128)(2,1)} %get-tuple-element.11.m_ref, bf16[3584,3584]{1,0:T(8,128)(2,1)} %get-tuple-element.12.wg_ref, bf16[3584,3584]{1,0:T(8,128)(2,1)} %get-tuple-element.13.wu_ref), custom_call_target="tpu_custom_call" | custom-call | flops 52613349376 | bytes 51380224 | tf_op jit(solution)/shard_map/gate_up/pallas_call | solution.py:699
  398.4 0.0 copy-start.2
  398.4 0.0 copy-start.3
  398.4 33.1 %convolution_convert_fusion.p_ref = bf16[1024,3584]{1,0:T(8,128)(2,1)} fusion(bf16[1024,3584]{1,0:T(8,128)(2,1)} %gate_up.1, bf16[3584,3584]{1,0:T(8,128)(2,1)} %get-tuple-element.14), kind=kOutput, calls=%fused_computation | convolution fusion | flops 26310344704 | bytes 40370176 | tf_op jit(solution)/shard_map/dot_general | solution.py:728
  431.5 0.0 copy-done.2
  431.5 0.0 copy-done.3
  431.5 9.8 %copy_bitcast_fusion = (bf16[1024,2,256]{2,1,0:T(2,128)(2,1)}, bf16[1024,2,256]{2,1,0:T(2,128)(2,1)}) fusion(bf16[2,1024,256]{2,1,0:T(8,128)(2,1)S(1)} %copy-done.3, bf16[2,1024,256]{2,1,0:T(8,128)(2,1)S(1)} %copy-done.2), kind=kLoop, calls=%fused_computation.2 | loop fusion | bytes 4194304 | tf_op jit(solution)/shard_map/transpose | solution.py:729
  441.2 183.7 %last.1 = (bf16[4096,896]{1,0:T(8,128)(2,1)}, bf16[4096,2,256]{2,1,0:T(2,128)(2,1)}, bf16[4096,2,256]{2,1,0:T(2,128)(2,1)}) custom-call(bf16[1024,3584]{1,0:T(8,128)(2,1)} %convolution_convert_fusion.p_ref, bf16[512,3584]{1,0:T(8,128)(2,1)} %get-tuple-element.15.h_ref, f32[8,3584]{1,0:T(8,128)} %get-tuple-element.16.n4_ref, ...), custom_call_target="tpu_custom_call" | custom-call | tf_op jit(solution)/shard_map/last/pallas_call | solution.py:683
  624.9 0.0 copy-start.1
  624.9 6.9 %copy.29 = bf16[4096,896]{1,0:T(8,128)(2,1)} copy(bf16[4096,896]{1,0:T(8,128)(2,1)} %get-tuple-element.28) | data formatting | bytes 14680064
  631.8 0.0 copy-done.1
  631.8 0.0 copy-start
  631.8 2.1 copy.30
  634.0 1.6 copy-done
  635.5 2.0 copy.31
  (1 shorter events, 0.0 us)
Async XLA Ops:
  4.1 11.5 %copy-start.4 = (s32[1,1024]{1,0:T(1,128)}, s32[1,1024]{1,0:T(1,128)S(1)}, u32[]{:S(2)}) copy-start(s32[1,1024]{1,0:T(1,128)S(1)} %get-tuple-element.20.pos_row_ref) | copy-start | bytes 12292
  398.4 33.1 %copy-start.2 = (bf16[2,1024,256]{2,1,0:T(8,128)(2,1)S(1)}, bf16[2,1024,256]{2,1,0:T(8,128)(2,1)}, u32[]{:S(2)}) copy-start(bf16[2,1024,256]{2,1,0:T(8,128)(2,1)} %get-tuple-element.17) | copy-start | bytes 3145732
  398.4 33.1 %copy-start.3 = (bf16[2,1024,256]{2,1,0:T(8,128)(2,1)S(1)}, bf16[2,1024,256]{2,1,0:T(8,128)(2,1)}, u32[]{:S(2)}) copy-start(bf16[2,1024,256]{2,1,0:T(8,128)(2,1)} %get-tuple-element.18) | copy-start | bytes 3145732
  624.9 6.9 %copy-start.1 = (bf16[4096,2,256]{2,1,0:T(2,128)(2,1)S(1)}, bf16[4096,2,256]{2,1,0:T(2,128)(2,1)}, u32[]{:S(2)}) copy-start(bf16[4096,2,256]{2,1,0:T(2,128)(2,1)} %get-tuple-element.29) | copy-start | bytes 12582916
  631.8 3.7 copy-start

commit v3 on v2

--- a/solution.py
+++ b/solution.py
@@ -17,7 +17,7 @@
 CHUNK = 16
 LAG = 2
 LINE = 4
-VMEM_BYTES = 62 * 1024 * 1024
+VMEM_BYTES = 67043328
 
 ANY = pl.BlockSpec(memory_space=pl.ANY)
 VMEM = pl.BlockSpec(memory_space=pltpu.VMEM)
@@ -205,7 +205,7 @@
 
             self.emit(self.out_rows(d, c))
 
-    def run(self, actions):
+    def run(self, actions, each):
         def body(t, carry):
             for turn in sorted(actions):
 
@@ -214,6 +214,7 @@
                     for action in actions[turn]:
                         action()
 
+            each(t)
             self.step(t)
             return carry
 
@@ -249,7 +250,7 @@
     return jnp.concatenate([lower * cos_tab - upper * sin_tab, upper * cos_tab + lower * sin_tab], axis=-1).astype(BF16)
 
 
-def front_kernel(scale, kv_heads, head_dim, x_ref, n_ref, wqkv_ref, wo_ref, wg_ref, wu_ref, wd_ref, cos_ref, sin_ref, pos_col_ref, pos_row_ref, m_ref, h_ref, k_out_ref, v_out_ref, gain_ref, wgf_ref, wuf_ref, wdf_ref, xm_buf, w_buf, wo_buf, qkv_buf, o_buf, p_buf, got, res_buf, n_buf, x_send, x_recv, n_send, n_recv, z_send, z_recv, own_send, own_recv, w_send, w_recv, load_sem, keep_load, keep_store, m_sem, h_sem, kv_sem, sum_send, sum_recv, out_send, out_recv):
+def layer_kernel(scale, kv_heads, head_dim, x_ref, n_ref, wq_ref, wk_ref, wv_ref, wo_ref, wg_ref, wu_ref, wd_ref, cos_ref, sin_ref, pos_col_ref, pos_row_ref, y_ref, kf_ref, vf_ref, wgf_ref, wuf_ref, wdf_ref, xm_buf, w_buf, wo_buf, qkv_buf, p_buf, got, res_buf, n_buf, gain_buf, wq_buf, wk_buf, wv_buf, k_buf, v_buf, x_send, x_recv, n_send, n_recv, z_send, z_recv, own_send, own_recv, w_send, w_recv, load_sem, keep_load, keep_store, tile_sem, kv_store, kv_send, kv_recv, fin_send, fin_recv, fin_own, *line_sems):
     row, line, me, mate, across, cross = places()
     seq, dim = xm_buf.shape
     cols = dim // 4
@@ -259,9 +260,10 @@
     heads = wo_ref.shape[0] // head_dim
     group = heads // kv_heads
     mine = pl.ds(pl.multiple_of(me * cols, cols), cols)
-    shards = [Shard(wqkv_ref, w_buf, True, 4), Shard(wo_ref, wo_buf, False, 2), Shard(wg_ref, wgf_ref, True, 4), Shard(wu_ref, wuf_ref, True, 4), Shard(wd_ref, wdf_ref, False, 4)]
+    own_rows = w_buf.at[pl.ds(pl.multiple_of(me * cols, cols), cols)]
+    shards = [Shard(own_rows, w_buf, True, 4), Shard(wo_ref, wo_buf, False, 2), Shard(wg_ref, wgf_ref, True, 4), Shard(wu_ref, wuf_ref, True, 4), Shard(wd_ref, wdf_ref, False, 4)]
     gather = WeightGather(shards, own_send, own_recv, w_send, w_recv)
-    first, out_first, ffw_first, units = 0, 4, 6, 18
+    units = 18
     peers = (mate, across, cross)
 
     def x_copy(hop, s):
@@ -323,10 +325,29 @@
     n_arrivals = [remote(n_ref, n_buf.at[dev], n_send.at[i], n_recv.at[i], {'dm': dev}) for i, dev in enumerate(peers)]
     loads = [
         pltpu.make_async_copy(x_ref.at[pl.ds(pl.multiple_of(me * seq, seq), seq)], xm_buf.at[:, mine], load_sem.at[0]),
-        pltpu.make_async_copy(wqkv_ref, shards[0].whole(me), load_sem.at[1]),
-        pltpu.make_async_copy(wo_ref, shards[1].whole(me), load_sem.at[2]),
-        pltpu.make_async_copy(n_ref, n_buf.at[me], load_sem.at[3]),
+        pltpu.make_async_copy(wo_ref, shards[1].whole(me), load_sem.at[1]),
+        pltpu.make_async_copy(n_ref, n_buf.at[me], load_sem.at[2]),
     ]
+    thirds = ((wq_ref, wq_buf), (wk_ref, wk_buf), (wv_ref, wv_buf))
+    third_loads = [pltpu.make_async_copy(src, buf, load_sem.at[3 + i]) for i, (src, buf) in enumerate(thirds)]
+
+    def flatten_own():
+        for load in third_loads:
+            load.wait()
+        flat_rows = min(cols, 64)
+
+        def body(i, carry):
+            part = pl.ds(pl.multiple_of(i * flat_rows, flat_rows), flat_rows)
+            there = pl.ds(pl.multiple_of(me * cols + i * flat_rows, flat_rows), flat_rows)
+            start = 0
+            for _, buf in thirds:
+                wide = buf.shape[1] * buf.shape[2]
+                w_buf[there, start:start + wide] = buf[part].reshape(flat_rows, wide)
+                start += wide
+            return carry
+
+        lax.fori_loop(0, cols // flat_rows, body, 0)
+
     rows = wg_ref.shape[0]
     down_rows = wd_ref.shape[0] // 4
     keeps = []
@@ -352,6 +373,8 @@
         for copy in keep(i, True):
             copy.wait()
 
+    for load in third_loads:
+        load.start()
     meet([{'dm': mate}, {'dm': across}, {'dm': cross}, {'dp': 1 - row}] + line_peers(line))
     for s in range(2):
         x_copy(1, s).start()
@@ -359,9 +382,10 @@
     x_copy(0, 0).start()
     for copy in n_copies:
         copy.start()
-    gather.start()
     for load in loads:
         load.start()
+    flatten_own()
+    gather.start()
     keep_load_start(0)
     z_first(0)
     keep_store_start(0)
@@ -389,7 +413,7 @@
     for load in loads:
         load.wait()
     for shard in range(4):
-        gain_ref[:, shard * cols:(shard + 1) * cols] = 1.0 + n_buf[shard]
+        gain_buf[:, shard * cols:(shard + 1) * cols] = 1.0 + n_buf[shard]
     x_arrival(0, 0).wait_recv()
     z_step(3, 1)
     gather.pass_x(3)
@@ -411,7 +435,7 @@
 
     def norm_body(i, carry):
         part = pl.ds(pl.multiple_of(i * norm_rows, norm_rows), norm_rows)
-        xm_buf[part, :] = unit_rows(xm_buf[part, :].astype(F32), gain_ref[0:1, :]).astype(BF16)
+        xm_buf[part, :] = unit_rows(xm_buf[part, :].astype(F32), gain_buf[0:1, :]).astype(BF16)
         return carry
 
     lax.fori_loop(0, seq // norm_rows, norm_body, 0)
@@ -441,13 +465,15 @@
         return carry
 
     lax.fori_loop(0, heads + kv_heads, rotate_body, 0)
-    kv_copies = []
-    for i in range(kv_heads):
-        for n, ref in enumerate((k_out_ref, v_out_ref)):
-            start = (heads + n * kv_heads + i) * head_dim
-            kv_copies.append(pltpu.make_async_copy(qkv_buf.at[:, pl.ds(start, head_dim)], ref.at[i], kv_sem.at[n, i]))
-    for copy in kv_copies:
-        copy.start()
+    def cache_body(i, carry):
+        part = pl.ds(pl.multiple_of(i * norm_rows, norm_rows), norm_rows)
+        wide = kv_heads * head_dim
+        for n, buf in enumerate((k_buf, v_buf)):
+            start = heads * head_dim + n * wide
+            buf[part] = qkv_buf[part, start:start + wide].reshape(norm_rows, kv_heads, head_dim)
+        return carry
+
+    lax.fori_loop(0, seq // norm_rows, cache_body, 0)
 
     block = seq // 8
     d_tile = min(dim, 512)
@@ -467,7 +493,7 @@
             capped = SOFT_CAP * jnp.tanh(scores * scale / SOFT_CAP)
             weights = jnp.where(allowed, jnp.exp(capped), 0.0)
             probs = (weights / jnp.sum(weights, axis=-1, keepdims=True)).astype(BF16)
-            o_buf[part, q_cols] = jnp.dot(probs, qkv_buf[:span, v_cols], preferred_element_type=F32).astype(BF16)
+            qkv_buf[part, q_cols] = jnp.dot(probs, qkv_buf[:span, v_cols], preferred_element_type=F32).astype(BF16)
             return carry
 
         lax.fori_loop(0, heads, head_body, 0)
@@ -477,7 +503,7 @@
 
         def out_body(n, carry):
             column = pl.ds(pl.multiple_of(n * d_tile, d_tile), d_tile)
-            p_buf[part, column] = jnp.dot(o_buf[part, :], wo_buf[:, column], preferred_element_type=F32).astype(BF16)
+            p_buf[part, column] = jnp.dot(qkv_buf[part, :heads * head_dim], wo_buf[:, column], preferred_element_type=F32).astype(BF16)
             return carry
 
         lax.fori_loop(0, dim // d_tile, out_body, 0)
@@ -490,14 +516,11 @@
     gather.pass_y(7)
 
     def finish(out_rows, rows, total):
-        hidden = (res_buf[rows, :].astype(F32) + unit_rows(total.astype(F32), gain_ref[1:2, :])).astype(BF16)
+        hidden = (res_buf[rows, :].astype(F32) + unit_rows(total.astype(F32), gain_buf[1:2, :])).astype(BF16)
         res_buf[rows, :] = hidden
-        xm_buf[out_rows, :] = unit_rows(hidden.astype(F32), gain_ref[2:3, :]).astype(BF16)
-
-    def emit(out_rows):
-        pltpu.make_async_copy(xm_buf.at[out_rows], m_ref.at[out_rows], m_sem).start()
-
-    sums = LineSum(p_buf, got, xm_buf, sum_send, sum_recv, out_send, out_recv, finish, emit)
+        xm_buf[out_rows, :] = unit_rows(hidden.astype(F32), gain_buf[2:3, :]).astype(BF16)
+
+    sums = LineSum(p_buf, got, xm_buf, *line_sems[:4], finish, lambda out_rows: None)
 
     ahead = block // CHUNK
     actions = {}
@@ -512,112 +535,157 @@
     for i in range(1, 4):
         at(i * ahead - (5 * ahead) // 8, functools.partial(both, i))
         at(i * ahead - (3 * ahead) // 8, functools.partial(both, 4 + i))
+
+    hidden_cols = wgf_ref.shape[1]
+    tile = min(hidden_cols // 2, 512)
+    tiles = hidden_cols // tile
+    span_rows = half // 4
+    z_buf = wo_buf
+
+    def group_rows(g):
+        return [pl.ds(pl.multiple_of(d * half + g * span_rows, span_rows), span_rows) for d in range(2)]
+
+    def slot_cols(slot):
+        return pl.ds(pl.multiple_of(slot * tile, tile), tile)
+
+    def gate_loads(i):
+        column = pl.ds(pl.multiple_of(lax.rem(i, tiles) * tile, tile), tile)
+        slot = 2 * lax.rem(i, 2)
+        return [pltpu.make_async_copy(ref.at[:, column], w_buf.at[:, slot_cols(slot + n)], tile_sem.at[slot + n]) for n, ref in enumerate((wgf_ref, wuf_ref))]
+
+    def gate_item(i):
+        for load in gate_loads(i):
+            load.wait()
+
+        @pl.when(i + 1 < 4 * tiles)
+        def _():
+            for load in gate_loads(i + 1):
+                load.start()
+
+        slot = 2 * lax.rem(i, 2)
+        parts = group_rows(lax.div(i, tiles))
+        column = pl.ds(pl.multiple_of(lax.rem(i, tiles) * tile, tile), tile)
+        ffw_in = jnp.concatenate([xm_buf[part, :] for part in parts], axis=0)
+        gate = jnp.dot(ffw_in, w_buf[:, slot_cols(slot)], preferred_element_type=F32).astype(BF16).astype(F32)
+        up = jnp.dot(ffw_in, w_buf[:, slot_cols(slot + 1)], preferred_element_type=F32).astype(BF16).astype(F32)
+        gated = (jax.nn.gelu(gate, approximate=True) * up).astype(BF16)
+        for d, part in enumerate(parts):
+            z_buf[part, column] = gated[d * span_rows:(d + 1) * span_rows]
+
+    ready = [(g + 1) * (sums.chunks // 4) + 6 * LAG for g in range(3)]
+    gate_start = max(max(ready[g] - (tiles * g) // 2 for g in range(3)), int(29 * sums.steps / 44))
+    gate_inside = max(0, min(3 * tiles, 2 * (sums.steps - gate_start)))
+
+    def open_gate():
+        gather.settle_units(range(6, 14), [2, 3])
+        for load in gate_loads(0):
+            load.start()
+
     turn = sums.steps / 44.0
-    y_turns = (8, 11, 15, 18, 22, 25, 29, 32, 36, 41)
+    y_turns = (8, 11, 15, 18, 22, 25, 29, 31, 34, 37)
     for k in range(8, units):
         at(int(y_turns[k - 8] * turn), functools.partial(gather.pass_y, k))
-    x_turns = (4, 9, 12, 16, 19, 23, 26, 30, 33, 38, 43)
-    for k in range(6, units - 1):
+    x_turns = (4, 9, 12, 16, 19, 23, 26, 28, 31, 34, 37, 40)
+    for k in range(6, units):
         at(int(x_turns[k - 6] * turn), functools.partial(gather.pass_x, k))
-    sums.run(actions)
-    gather.pass_x(units - 1)
-
-    h_store = pltpu.make_async_copy(res_buf, h_ref, h_sem)
-    ends = (line == 0) | (line == LINE - 1)
-
-    @pl.when(ends)
-    def _():
-        h_store.start()
-
-    pltpu.make_async_copy(xm_buf, m_ref, m_sem).wait()
+    at(gate_start, open_gate)
+
+    def each_first(t):
+        for n in range(2):
+            i = 2 * (t - gate_start) + n
+
+            @pl.when((i >= 0) & (i < gate_inside))
+            def _():
+                gate_item(i)
+
+    sums.run(actions, each_first)
+
+    def gate_body(i, carry):
+        gate_item(i)
+        return carry
+
+    lax.fori_loop(gate_inside, 4 * tiles, gate_body, 0)
     sums.settle()
-    gather.settle_units(range(6, units), [2, 3, 4])
-    for copy in kv_copies:
-        copy.wait()
-    for copy in n_copies:
-        copy.wait_send()
-    x_copy(0, 0).wait_send()
-    for s in range(2):
-        x_copy(1, s).wait_send()
-        x_copy(2, s).wait_send()
-
-    @pl.when(ends)
-    def _():
-        h_store.wait()
-
-
-def last_kernel(p_ref, h_ref, n4_ref, k_ref, v_ref, y_ref, kf_ref, vf_ref, p_buf, got, y_buf, res_buf, k_buf, v_buf, res_sem, kv_load, kv_store, kv_send, kv_recv, fin_send, fin_recv, own_sem, p_sem, sum_send, sum_recv, out_send, out_recv):
-    row, line, me, mate, across, cross = places()
-    seq = p_ref.shape[0]
-    cols = y_ref.shape[1]
-    res_load = pltpu.make_async_copy(h_ref, res_buf, res_sem)
-    p_load = pltpu.make_async_copy(p_ref, p_buf, p_sem)
-    ends = (line == 0) | (line == LINE - 1)
-    caches = ((k_ref, kf_ref, k_buf), (v_ref, vf_ref, v_buf))
-
-    def block(ref, shard):
+    gather.settle_units(range(14, units), [4])
+
+    d_tiles = dim // tile
+
+    def down_load(i):
+        column = pl.ds(pl.multiple_of(lax.rem(i, d_tiles) * tile, tile), tile)
+        slot = lax.rem(i, 4)
+        return pltpu.make_async_copy(wdf_ref.at[:, column], w_buf.at[:, slot_cols(slot)], tile_sem.at[slot])
+
+    def down_item(i):
+        down_load(i).wait()
+
+        @pl.when(i + 2 < 4 * d_tiles)
+        def _():
+            down_load(i + 2).start()
+
+        parts = group_rows(lax.div(i, d_tiles))
+        column = pl.ds(pl.multiple_of(lax.rem(i, d_tiles) * tile, tile), tile)
+        gated = jnp.concatenate([z_buf[part, :] for part in parts], axis=0)
+        down = jnp.dot(gated, w_buf[:, slot_cols(lax.rem(i, 4))], preferred_element_type=F32).astype(BF16)
+        for d, part in enumerate(parts):
+            p_buf[part, column] = down[d * span_rows:(d + 1) * span_rows]
+
+    down_load(0).start()
+    down_load(1).start()
+
+    caches = ((k_buf, kf_ref), (v_buf, vf_ref))
+
+    def rows_of(ref, shard):
         return ref.at[pl.ds(pl.multiple_of(shard * seq, seq), seq)]
 
     def kv_copy(i, hop):
-        src, dst, _ = caches[i]
+        src, dst = caches[i]
         if hop == 0:
-            return remote(src, block(dst, me), kv_send.at[i, hop], kv_recv.at[i, hop], {'dm': across})
+            return remote(src, rows_of(dst, me), kv_send.at[i, hop], kv_recv.at[i, hop], {'dm': across})
         if hop == 1:
-            return remote(src, block(dst, me), kv_send.at[i, hop], kv_recv.at[i, hop], {'dm': mate})
-        return remote(block(dst, across), block(dst, across), kv_send.at[i, hop], kv_recv.at[i, hop], {'dm': mate})
+            return remote(src, rows_of(dst, me), kv_send.at[i, hop], kv_recv.at[i, hop], {'dm': mate})
+        return remote(rows_of(dst, across), rows_of(dst, across), kv_send.at[i, hop], kv_recv.at[i, hop], {'dm': mate})
 
     def kv_arrival(i, hop):
-        region = block(caches[i][1], (across, mate, cross)[hop])
+        region = rows_of(caches[i][1], (across, mate, cross)[hop])
         return remote(region, region, kv_send.at[i, hop], kv_recv.at[i, hop], {'dm': mate})
 
-    kv_loads = [pltpu.make_async_copy(src, buf, kv_load.at[i]) for i, (src, _, buf) in enumerate(caches)]
-    kv_stores = [pltpu.make_async_copy(buf, block(dst, me), kv_store.at[i]) for i, (_, dst, buf) in enumerate(caches)]
-
-    def column(shard):
-        return pl.ds(pl.multiple_of(shard * cols, cols), cols)
-
-    def finish(out_rows, rows, total):
-        y_buf[out_rows, :] = (res_buf[rows, :].astype(F32) + unit_rows(total.astype(F32), n4_ref[3:4, :])).astype(BF16)
-
-    def emit(out_rows):
-        start = out_rows.start
-        there = pl.ds(pl.multiple_of(me * seq + start, CHUNK), CHUNK)
-        for i, dev in enumerate((across, cross, mate)):
-            remote(y_buf.at[out_rows, column(dev)], y_ref.at[there], fin_send.at[i], fin_recv.at[i], {'dm': dev}).start()
-        pltpu.make_async_copy(y_buf.at[out_rows, column(me)], y_ref.at[there], own_sem).start()
-
-    sums = LineSum(p_buf, got, y_buf, sum_send, sum_recv, out_send, out_recv, finish, emit)
-
-    p_load.start()
-    meet([{'dm': mate}, {'dm': across}, {'dm': cross}] + line_peers(line))
-
-    @pl.when(ends)
-    def _():
-        res_load.start()
-
+    kv_stores = [pltpu.make_async_copy(src, rows_of(dst, me), kv_store.at[i]) for i, (src, dst) in enumerate(caches)]
     for i in range(2):
-        kv_loads[i].start()
         kv_copy(i, 0).start()
         kv_copy(i, 1).start()
-
-    @pl.when(ends)
-    def _():
-        res_load.wait()
-
-    p_load.wait()
-
-    def keep_own():
-        for i in range(2):
-            kv_loads[i].wait()
-            kv_stores[i].start()
+        kv_stores[i].start()
+
+    def down_body(i, carry):
+        down_item(i)
+        return carry
+
+    lax.fori_loop(0, d_tiles, down_body, 0)
+
+    def column_of(shard):
+        return pl.ds(pl.multiple_of(shard * cols, cols), cols)
+
+    def finish_last(out_rows, rows, total):
+        xm_buf[out_rows, :] = (res_buf[rows, :].astype(F32) + unit_rows(total.astype(F32), gain_buf[3:4, :])).astype(BF16)
+
+    def emit_last(out_rows):
+        there = pl.ds(pl.multiple_of(me * seq + out_rows.start, CHUNK), CHUNK)
+        for i, dev in enumerate((across, cross, mate)):
+            remote(xm_buf.at[out_rows, column_of(dev)], y_ref.at[there], fin_send.at[i], fin_recv.at[i], {'dm': dev}).start()
+        pltpu.make_async_copy(xm_buf.at[out_rows, column_of(me)], y_ref.at[there], fin_own).start()
+
+    last_sums = LineSum(p_buf, got, xm_buf, *line_sems[4:], finish_last, emit_last)
 
     def pass_kv(i):
         kv_arrival(i, 0).wait_recv()
         kv_copy(i, 2).start()
 
-    actions = {1: [keep_own], min(14, sums.steps - 2): [functools.partial(pass_kv, 0)], min(17, sums.steps - 1): [functools.partial(pass_kv, 1)]}
-    sums.run(actions)
-    sums.settle()
+    def each_last(t):
+        @pl.when(t < 3 * d_tiles)
+        def _():
+            down_item(t + d_tiles)
+
+    last_sums.run({min(14, sums.steps - 2): [functools.partial(pass_kv, 0)], min(17, sums.steps - 1): [functools.partial(pass_kv, 1)]}, each_last)
+    last_sums.settle()
     for i in range(2):
         kv_stores[i].wait()
         for hop in range(3):
@@ -625,23 +693,16 @@
         kv_arrival(i, 1).wait_recv()
         kv_arrival(i, 2).wait_recv()
     for i, dev in enumerate((across, cross, mate)):
-        done = remote(y_buf.at[:, column(dev)], block(y_ref, dev), fin_send.at[i], fin_recv.at[i], {'dm': dev})
+        done = remote(xm_buf.at[:, column_of(dev)], rows_of(y_ref, dev), fin_send.at[i], fin_recv.at[i], {'dm': dev})
         done.wait_send()
         done.wait_recv()
-    pltpu.make_async_copy(y_buf.at[:, column(me)], block(y_ref, me), own_sem).wait()
-
-
-def gate_kernel(m_ref, wg_ref, wu_ref, z_ref):
-    block = min(m_ref.shape[0], 512)
-
-    def body(i, carry):
-        rows = pl.ds(pl.multiple_of(i * block, block), block)
-        gate = jnp.dot(m_ref[rows, :], wg_ref[...], preferred_element_type=F32).astype(BF16).astype(F32)
-        up = jnp.dot(m_ref[rows, :], wu_ref[...], preferred_element_type=F32).astype(BF16).astype(F32)
-        z_ref[rows, :] = (jax.nn.gelu(gate, approximate=True) * up).astype(BF16)
-        return carry
-
-    lax.fori_loop(0, m_ref.shape[0] // block, body, 0)
+    pltpu.make_async_copy(xm_buf.at[:, column_of(me)], rows_of(y_ref, me), fin_own).wait()
+    for copy in n_copies:
+        copy.wait_send()
+    x_copy(0, 0).wait_send()
+    for s in range(2):
+        x_copy(1, s).wait_send()
+        x_copy(2, s).wait_send()
 
 
 def like(*shape, dtype=BF16):
@@ -652,60 +713,30 @@
     return pltpu.CompilerParams(collective_id=collective_id, has_side_effects=True, vmem_limit_bytes=VMEM_BYTES)
 
 
-def line_scratch(seq, dim):
-    chunks = seq // 2 // CHUNK
-    return [DMA((2, chunks))] * 4
-
-
-def front(x, norms, wqkv, wo, wg, wu, wd, cos_tab, sin_tab, pos, scale, kv_heads, head_dim):
+def run_layer(x, norms, wq, wk, wv, wo, wg, wu, wd, cos_tab, sin_tab, pos, scale):
     seq = pos.shape[0]
     cols = x.shape[1]
     dim = 4 * cols
-    width = wqkv.shape[1]
+    kv_heads, head_dim = wk.shape[1:]
+    width = wo.shape[0] + 2 * kv_heads * head_dim
     units = 18
+    chunks = seq // 2 // CHUNK
+    cache = (seq, kv_heads, head_dim)
     return pl.pallas_call(
-        functools.partial(front_kernel, scale, kv_heads, head_dim),
-        name='front',
-        out_shape=(like(seq, dim), like(seq // 2, dim), like(kv_heads, seq, head_dim), like(kv_heads, seq, head_dim), like(8, dim, dtype=F32), like(4 * wg.shape[0], wg.shape[1]), like(4 * wu.shape[0], wu.shape[1]), like(wd.shape[0], 4 * wd.shape[1])),
-        in_specs=[ANY] * 7 + [VMEM] * 4,
-        out_specs=(ANY,) * 4 + (VMEM,) + (ANY,) * 3,
+        functools.partial(layer_kernel, scale, kv_heads, head_dim),
+        name='layer',
+        out_shape=(like(4 * seq, cols), like(4 * seq, kv_heads, head_dim), like(4 * seq, kv_heads, head_dim), like(4 * wg.shape[0], wg.shape[1]), like(4 * wu.shape[0], wu.shape[1]), like(wd.shape[0], 4 * wd.shape[1])),
+        in_specs=[ANY] * 9 + [VMEM] * 4,
+        out_specs=(ANY,) * 6,
         scratch_shapes=[
-            pltpu.VMEM((seq, dim), BF16), pltpu.VMEM((dim, width), BF16), pltpu.VMEM((wo.shape[0], dim), BF16), pltpu.VMEM((seq, width), BF16), pltpu.VMEM((seq, wo.shape[0]), BF16),
-            pltpu.VMEM((seq, dim), BF16), pltpu.VMEM((2, seq // 2, dim), BF16), pltpu.VMEM((seq // 2, dim), BF16), pltpu.VMEM((4,) + norms.shape, F32),
-            DMA((3, 2)), DMA((3, 2)), DMA((3,)), DMA((3,)), DMA((2, 2 * LINE)), DMA((2 * LINE,)), DMA((5,)), DMA((5,)), DMA((units, 4)), DMA((units, 4)), DMA((4,)), DMA((4,)), DMA((4,)), DMA, DMA, DMA((2, kv_heads)),
-        ] + line_scratch(seq, dim),
+            pltpu.VMEM((seq, dim), BF16), pltpu.VMEM((dim, width), BF16), pltpu.VMEM((wo.shape[0], dim), BF16), pltpu.VMEM((seq, width), BF16),
+            pltpu.VMEM((seq, dim), BF16), pltpu.VMEM((2, seq // 2, dim), BF16), pltpu.VMEM((seq // 2, dim), BF16), pltpu.VMEM((4,) + norms.shape, F32), pltpu.VMEM((8, dim), F32),
+            pltpu.VMEM(wq.shape, BF16), pltpu.VMEM(wk.shape, BF16), pltpu.VMEM(wv.shape, BF16), pltpu.VMEM(cache, BF16), pltpu.VMEM(cache, BF16),
+            DMA((3, 2)), DMA((3, 2)), DMA((3,)), DMA((3,)), DMA((2, 2 * LINE)), DMA((2 * LINE,)), DMA((5,)), DMA((5,)), DMA((units, 4)), DMA((units, 4)), DMA((6,)), DMA((4,)), DMA((4,)),
+            DMA((4,)), DMA((2,)), DMA((2, 3)), DMA((2, 3)), DMA((3,)), DMA((3,)), DMA,
+        ] + [DMA((2, chunks))] * 8,
         compiler_params=params(0),
-    )(x, norms, wqkv, wo, wg, wu, wd, cos_tab, sin_tab, pos[:, None], pos[None, :])
-
-
-def last(part, hidden, gains, k_own, v_own):
-    seq, dim = part.shape
-    return pl.pallas_call(
-        last_kernel,
-        name='last',
-        out_shape=(like(4 * seq, dim // 4), like(4 * seq, *k_own.shape[1:]), like(4 * seq, *v_own.shape[1:])),
-        in_specs=[ANY, ANY, VMEM, ANY, ANY],
-        out_specs=(ANY,) * 3,
-        scratch_shapes=[pltpu.VMEM((seq, dim), BF16), pltpu.VMEM((2, seq // 2, dim), BF16), pltpu.VMEM((seq, dim), BF16), pltpu.VMEM((seq // 2, dim), BF16), pltpu.VMEM(k_own.shape, BF16), pltpu.VMEM(v_own.shape, BF16), DMA, DMA((2,)), DMA((2,)), DMA((2, 3)), DMA((2, 3)), DMA((3,)), DMA((3,)), DMA, DMA] + line_scratch(seq, dim),
-        compiler_params=params(2),
-    )(part, hidden, gains, k_own, v_own)
-
-
-def gate_up(m, wg, wu):
-    seq, dim = m.shape
-    hidden = wg.shape[1]
-    tile = min(hidden, 512)
-    w_spec = pl.BlockSpec((dim, tile), lambda f: (0, f))
-    return pl.pallas_call(
-        gate_kernel,
-        name='gate_up',
-        grid=(hidden // tile,),
-        out_shape=like(seq, hidden),
-        in_specs=[pl.BlockSpec((seq, dim), lambda f: (0, 0)), w_spec, w_spec],
-        out_specs=pl.BlockSpec((seq, tile), lambda f: (0, f)),
-        compiler_params=pltpu.CompilerParams(vmem_limit_bytes=VMEM_BYTES),
-        cost_estimate=pl.CostEstimate(flops=4 * seq * dim * hidden, bytes_accessed=4 * dim * hidden, transcendentals=seq * hidden),
-    )(m, wg, wu)
+    )(x, norms, wq, wk, wv, wo, wg, wu, wd, cos_tab, sin_tab, pos[:, None], pos[None, :])
 
 
 def solution(mesh):
@@ -718,16 +749,12 @@
         scale = (dim / (heads * tp_size)) ** -0.5
         norms = jnp.stack([norm_pre_attn, norm_post_attn, norm_pre_ffw, norm_post_ffw]).astype(F32)
         norms = jnp.concatenate([norms, jnp.zeros_like(norms)])
-        wqkv = jnp.concatenate([w.reshape(w.shape[0], -1) for w in (w_query, w_key, w_value)], axis=1)
         pos = lax.dynamic_index_in_dim(positions, lax.axis_index('dm'), 0, keepdims=False)
         half_dim = head_dim // 2
         inv_freq = ROPE_BASE ** (-2.0 * jnp.arange(half_dim, dtype=F32) / head_dim)
         angles = pos.astype(F32)[:, None] * inv_freq[None, :]
-        ffw_in, hidden, k_rot, v, gains, wg, wu, wd = front(tokens, norms, wqkv, w_out.reshape(heads * head_dim, cols), w_gate, w_up, w_down, jnp.cos(angles), jnp.sin(angles), pos, scale, w_key.shape[1], head_dim)
-        gated = gate_up(ffw_in, wg, wu)
-        down_part = jnp.dot(gated, wd, preferred_element_type=F32).astype(BF16)
-        k_own, v_own = jnp.swapaxes(k_rot, 0, 1), jnp.swapaxes(v, 0, 1)
-        return last(down_part, hidden, gains, k_own, v_own)
+        outs = run_layer(tokens, norms, w_query, w_key, w_value, w_out.reshape(heads * head_dim, cols), w_gate, w_up, w_down, jnp.cos(angles), jnp.sin(angles), pos, scale)
+        return outs[:3]
 
     width_spec = P('dm')
     in_specs = (P('dp', 'dm'), P('dp', None), width_spec, P('dm', 'tp', None), P('dm', 'tp', None), P('dm', 'tp', None), P('tp', None, 'dm'), width_spec, width_spec, P('dm', 'tp'), P('dm', 'tp'), P('tp', 'dm'), width_spec)

time: 638 us -> 563 us (0.88)
  matrix products: 33.1 us -> 0 us
  Pallas kernels: 566 us -> 541 us
  local copies, waits for them, and re-layouts: 30.8 us -> 16.4 us
    dot_general x1 -> x0, matrix products: 33.1 us -> none  [layer(): down_part = jnp.dot(gated, wd, preferred_element_type=F32).astype(BF16)]
    pallas_call x3 -> x1, Pallas kernels: 566 us -> 541 us  [run_layer(): pl.pallas_call(functools.partial(layer_kernel, scale, kv_heads, head_dim)...]
    transpose x1 -> x0, local copies, waits for them, and re-layouts: 9.79 us -> none  [layer(): k_own, v_own = (jnp.swapaxes(k_rot, 0, 1), jnp.swapaxes(v, 0, 1))]
    unnamed x16 -> x9, local copies, waits for them, and re-layouts: 17.3 us -> 12.6 us
where the time goes in v3:
time: 563 us; the launch traced here: 562 us
  Pallas kernels  541 us (96%)
  local copies, waits for them, and re-layouts  16.4 us (3%)
    pallas_call x1, Pallas kernels, run_layer(): pl.pallas_call(functools.partial(layer_kernel, scale, kv_heads, head_dim)...  541 us
    unnamed x9, local copies, waits for them, and re-layouts  12.6 us

profile of v3, /device:TPU:0, one launch (start us, length us, event | category | flops | bytes accessed | tf_op | source)
XLA Modules:
  0.0 562.3 jit_solution(21622789334041884)
XLA Ops:
  0.6 0.7 stack.15
  1.3 0.7 stack.16
  2.0 0.7 stack.17
  2.7 0.7 stack.18
  3.4 0.7 fusion.8
  4.1 0.0 copy-start.2
  4.1 0.6 fusion.7.n_ref
  4.8 0.0 copy-done.2
  4.8 1.0 copy.16.pos_col_ref
  5.8 3.0 multiply_sine_fusion
  8.8 540.9 %layer.1 = (bf16[4096,896]{1,0:T(8,128)(2,1)}, bf16[4096,2,256]{2,1,0:T(2,128)(2,1)}, bf16[4096,2,256]{2,1,0:T(2,128)(2,1)}, bf16[3584,3584]{1,0:T(8,128)(2,1)},...) custom-call(bf16[4096,896]{1,0:T(8,128)(2,1)} %x_ref.1, f32[8,896]{1,0:T(8,128)} %fusion.7.n_ref, ...), custom_call_target="tpu_custom_call" | custom-call | tf_op jit(solution)/shard_map/layer/pallas_call | solution.py:725
  549.7 0.0 copy-start.1
  549.7 6.9 %copy.20 = bf16[4096,896]{1,0:T(8,128)(2,1)} copy(bf16[4096,896]{1,0:T(8,128)(2,1)} %get-tuple-element.16) | data formatting | bytes 14680064
  556.6 0.0 copy-done.1
  556.6 0.0 copy-start
  556.6 2.1 copy.21
  558.7 1.6 copy-done
  560.3 2.0 copy.22
  (1 shorter events, 0.0 us)
Async XLA Ops:
  4.1 0.6 copy-start.2
  549.7 6.9 %copy-start.1 = (bf16[4096,2,256]{2,1,0:T(2,128)(2,1)S(1)}, bf16[4096,2,256]{2,1,0:T(2,128)(2,1)}, u32[]{:S(2)}) copy-start(bf16[4096,2,256]{2,1,0:T(2,128)(2,1)} %get-tuple-element.17) | copy-start | bytes 12582916
  556.6 3.7 copy-start
